TPU v7x, 32 devices: a whole 2x2x4 slice. The times are simulated.
32 devices in a mesh: vp: 4 (over z), dp: 8 (over y, x, core).
Axes of the slice: x: 2, y: 2, z: 4, core: 2. Of those that a mesh axis runs over, the one named last changes fastest.
Arguments:
- student_x: bfloat16 [5120, 384], P('dp')
- teacher_x: bfloat16 [1024, 384], P('dp')
- w_in: bfloat16 [384, 2048], replicated
- b_in: bfloat16 [2048], replicated
- w_mid: bfloat16 [2048, 2048], replicated
- b_mid: bfloat16 [2048], replicated
- w_out: bfloat16 [2048, 256], replicated
- b_out: bfloat16 [256], replicated
- protos: bfloat16 [256, 65536], P(None, 'vp')
- ema_w_in: bfloat16 [384, 2048], replicated
- ema_b_in: bfloat16 [2048], replicated
- ema_w_mid: bfloat16 [2048, 2048], replicated
- ema_b_mid: bfloat16 [2048], replicated
- ema_w_out: bfloat16 [2048, 256], replicated
- ema_b_out: bfloat16 [256], replicated
- ema_protos: bfloat16 [256, 65536], P(None, 'vp')
Outputs:
- output 1: float32 [], replicated
- output 2: float32 [384, 2048], replicated
- output 3: float32 [2048], replicated
- output 4: float32 [2048, 2048], replicated
- output 5: float32 [2048], replicated
- output 6: float32 [2048, 256], replicated
- output 7: float32 [256], replicated
- output 8: float32 [256, 65536], P(None, 'vp')
All inputs are finite; a program needn't handle non-finite values.
Results may differ from a plain program's by a relative error of at most 0.00519324.
Values sent between devices are 32-bit elements.
A program may use at most 1 GiB of HBM per device.

v0:
```python
import jax
import jax.numpy as jnp
from jax import lax
from jax.sharding import PartitionSpec as P

ALL_CROPS = 10
GLOBAL_CROPS = 2
SINK_ITERS = 3
TEMP_STUDENT = 0.1
TEMP_TEACHER = 0.04


def gelu_slope(pre):
    cdf = 0.5 * (1.0 + lax.erf(pre * 0.7071067811865476))
    return cdf + pre * jnp.exp(-0.5 * pre * pre) * 0.3989422804014327


def mlp_forward(feats, w_in, b_in, w_mid, b_mid, w_out, b_out):
    pre_one = jnp.dot(feats, w_in, preferred_element_type=jnp.float32) + b_in.astype(jnp.float32)
    hid_one = jax.nn.gelu(pre_one, approximate=False).astype(jnp.bfloat16)
    pre_two = jnp.dot(hid_one, w_mid, preferred_element_type=jnp.float32) + b_mid.astype(jnp.float32)
    hid_two = jax.nn.gelu(pre_two, approximate=False).astype(jnp.bfloat16)
    proj = jnp.dot(hid_two, w_out, preferred_element_type=jnp.float32) + b_out.astype(jnp.float32)
    inv_norm = lax.rsqrt(jnp.sum(proj * proj, axis=-1, keepdims=True))
    unit = proj * inv_norm
    return unit.astype(jnp.bfloat16), (pre_one, hid_one, pre_two, hid_two, unit, inv_norm)


def mlp_backward(g_emb, feats, saved, w_mid, w_out):
    pre_one, hid_one, pre_two, hid_two, unit, inv_norm = saved
    g_proj = (g_emb - unit * jnp.sum(unit * g_emb, axis=-1, keepdims=True)) * inv_norm
    g_proj_lo = g_proj.astype(jnp.bfloat16)
    g_w_out = jnp.einsum('nh,nb->hb', hid_two, g_proj_lo, preferred_element_type=jnp.float32)
    g_hid_two = jnp.einsum('nb,hb->nh', g_proj_lo, w_out, preferred_element_type=jnp.float32)
    g_pre_two = g_hid_two.astype(jnp.bfloat16).astype(jnp.float32) * gelu_slope(pre_two)
    g_pre_two_lo = g_pre_two.astype(jnp.bfloat16)
    g_w_mid = jnp.einsum('ng,nh->gh', hid_one, g_pre_two_lo, preferred_element_type=jnp.float32)
    g_hid_one = jnp.einsum('nh,gh->ng', g_pre_two_lo, w_mid, preferred_element_type=jnp.float32)
    g_pre_one = g_hid_one.astype(jnp.bfloat16).astype(jnp.float32) * gelu_slope(pre_one)
    g_w_in = jnp.einsum('nf,nh->fh', feats, g_pre_one.astype(jnp.bfloat16), preferred_element_type=jnp.float32)
    return (g_w_in, jnp.sum(g_pre_one, axis=0), g_w_mid, jnp.sum(g_pre_two, axis=0), g_w_out, jnp.sum(g_proj, axis=0))


def col_normalize(protos):
    proto_f = protos.astype(jnp.float32)
    inv_col = lax.rsqrt(jnp.sum(proto_f * proto_f, axis=0, keepdims=True))
    unit = proto_f * inv_col
    return unit.astype(jnp.bfloat16), unit, inv_col


def col_normalize_backward(g_unit, unit, inv_col):
    return (g_unit - unit * jnp.sum(unit * g_unit, axis=0, keepdims=True)) * inv_col


def pair_targets(q_three):
    pad_rows = ALL_CROPS - GLOBAL_CROPS
    return jnp.sum(q_three, axis=1, keepdims=True) - jnp.pad(q_three, ((0, 0), (0, pad_rows), (0, 0)))


def crop_counts():
    crop_idx = jnp.arange(ALL_CROPS)
    return (GLOBAL_CROPS - (crop_idx < GLOBAL_CROPS).astype(jnp.int32)).astype(jnp.float32)


def solution(mesh):
    vp_size = mesh.shape['vp']
    dp_size = mesh.shape['dp']

    def local_step(student_x, teacher_x, w_in, b_in, w_mid, b_mid, w_out, b_out, protos,
                   ema_w_in, ema_b_in, ema_w_mid, ema_b_mid, ema_w_out, ema_b_out, ema_protos):
        n_img = student_x.shape[0] // ALL_CROPS
        local_proto = protos.shape[1]
        n_proto = local_proto * vp_size
        n_rows = GLOBAL_CROPS * n_img * dp_size
        t_emb, _ = mlp_forward(teacher_x, ema_w_in, ema_b_in, ema_w_mid, ema_b_mid, ema_w_out, ema_b_out)
        t_unit = col_normalize(ema_protos)[0]
        q_mat = jnp.exp(jnp.dot(t_emb, t_unit, preferred_element_type=jnp.float32) / TEMP_TEACHER)
        q_mat = q_mat / lax.psum(jnp.sum(q_mat), ('vp', 'dp'))
        for _ in range(SINK_ITERS):
            proto_sum = lax.psum(jnp.sum(q_mat, axis=0, keepdims=True), 'dp')
            q_mat = q_mat / (proto_sum * n_proto)
            crop_sum = lax.psum(jnp.sum(q_mat, axis=1, keepdims=True), 'vp')
            q_mat = q_mat / (crop_sum * n_rows)
        q_three = (q_mat * n_rows).reshape(n_img, GLOBAL_CROPS, local_proto)

        s_emb, saved = mlp_forward(student_x, w_in, b_in, w_mid, b_mid, w_out, b_out)
        s_unit, unit_f, inv_col = col_normalize(protos)
        logits = jnp.dot(s_emb, s_unit, preferred_element_type=jnp.float32) / TEMP_STUDENT
        logits = logits.reshape(n_img, ALL_CROPS, local_proto)
        row_max = lax.pmax(jnp.max(logits, axis=-1, keepdims=True), 'vp')
        shifted = logits - row_max
        exp_s = jnp.exp(shifted)
        row_sum = lax.psum(jnp.sum(exp_s, axis=-1, keepdims=True), 'vp')
        scale = 1.0 / (n_img * dp_size * GLOBAL_CROPS * (ALL_CROPS - 1))
        targets = pair_targets(q_three)
        loss = lax.psum(jnp.sum(targets * (jnp.log(row_sum) - shifted)), ('vp', 'dp')) * scale
        g_logits = (crop_counts()[:, None] * (exp_s / row_sum) - targets) * (scale / TEMP_STUDENT)
        g_logits = g_logits.reshape(n_img * ALL_CROPS, local_proto).astype(jnp.bfloat16)
        g_emb = jnp.einsum('rk,bk->rb', g_logits, s_unit, preferred_element_type=jnp.float32)
        g_unit = lax.psum(jnp.einsum('rb,rk->bk', s_emb, g_logits, preferred_element_type=jnp.float32), 'dp')
        head_grads = lax.psum(mlp_backward(g_emb, student_x, saved, w_mid, w_out), ('vp', 'dp'))
        g_protos = col_normalize_backward(g_unit, unit_f, inv_col)
        return (loss,) + tuple(head_grads) + (g_protos,)

    by_rows = P('dp', None)
    by_cols = P(None, 'vp')
    replicated = P()
    head_specs = (replicated,) * 6
    in_specs = (by_rows, by_rows) + head_specs + (by_cols,) + head_specs + (by_cols,)
    out_specs = (replicated,) * 7 + (by_cols,)
    return jax.shard_map(local_step, mesh=mesh, in_specs=in_specs, out_specs=out_specs, check_vma=False)
```

profile of v0, /device:TPU:0, one launch (start us, length us, event | category | flops | bytes accessed | tf_op | source)
XLA Modules:
  0.0 1041.0 jit_solution(1282677709533965966)
XLA Ops:
  12.6 10.1 fusion.66
  23.1 10.4 %fusion.148 = (f32[]{:T(128)}, f32[128,16384]{1,0:T(8,128)}) fusion(bf16[256,16384]{1,0:T(8,128)(2,1)} %param.31, f32[16384]{0:T(1024)S(1)} %rsqrt.33, f32[128,256]{1,0:T(8,128)S(1)} %get-tuple-element.38, f32[128]{0:T(128)S(1)} %rsqrt.32), kind=kOutput, calls=%fused_computation.218 | convolution fusion | flops 1090584576 | bytes 16974340 | tf_op jit(solution)/shard_map/dot_general | solution.py:77
  33.5 42.3 %psum.112 = f32[]{:T(128)} all-reduce(f32[]{:T(128)} %get-tuple-element.39), channel_id=1, replica_groups=mesh['vp'=4,'dp'=8] {'vp','dp'}, use_global_device_ids=true, to_apply=%region_3.0 | all-reduce | flops 1 | bytes 8 | tf_op jit(solution)/shard_map/psum | solution.py:78
  75.9 5.3 divide_reduce_fusion
  81.3 5.3 fusion.9
  86.7 13.8 %fusion.29 = (bf16[640,2048]{1,0:T(8,128)(2,1)S(1)}, f32[640,2048]{1,0:T(8,128)}) fusion(f32[2048]{0:T(1024)S(1)} %convert_element_type.99, bf16[640,384]{1,0:T(8,128)(2,1)S(1)} %copy-done.17, bf16[384,2048]{1,0:T(8,128)(2,1)S(1)} %copy-done), kind=kOutput, calls=%fused_computation.44 | convolution fusion | flops 1093140480 | bytes 9936896 | tf_op jit(solution)/shard_map/dot_general | solution.py:19
  100.6 18.2 %fusion.32 = (bf16[640,2048]{1,0:T(8,128)(2,1)S(1)}, f32[640,2048]{1,0:T(8,128)}) fusion(f32[2048]{0:T(1024)S(1)} %convert_element_type.101, bf16[640,2048]{1,0:T(8,128)(2,1)S(1)} %get-tuple-element.41, bf16[2048,2048]{1,0:T(8,128)(2,1)S(1)} %bitcast.67), kind=kOutput, calls=%fused_computation.47 | convolution fusion | flops 5455216640 | bytes 18882560 | tf_op jit(solution)/shard_map/dot_general | solution.py:21
  121.3 18.4 %fusion.149 = (f32[640]{0:T(1024)S(1)}, f32[640,16384]{1,0:T(8,128)}) fusion(bf16[256,16384]{1,0:T(8,128)(2,1)} %param.24, f32[16384]{0:T(1024)S(1)} %rsqrt.35, f32[640,256]{0,1:T(8,128)S(1)} %get-tuple-element.46, f32[640]{0:T(1024)S(1)} %rsqrt.34), kind=kOutput, calls=%fused_computation.219 | convolution fusion | flops 5402590720 | bytes 51057664 | tf_op jit(solution)/shard_map/dot_general | solution.py:88
  140.5 18.4 %pmax.7 = f32[64,10,1]{1,0,2:T(8,128)S(1)} all-reduce(f32[64,10,1]{1,0,2:T(8,128)S(1)} %broadcast_in_dim.43), channel_id=1, replica_groups=mesh['vp'=4,'dp'=8] {'vp'}, use_global_device_ids=true, to_apply=%region_20.0 | all-reduce | flops 640 | bytes 5120 | tf_op jit(solution)/shard_map/pmax | solution.py:90
  164.0 8.4 psum.114
  172.4 5.5 fusion.20
  178.0 16.8 %exponential_reduce_fusion = f32[640]{0:T(1024)S(1)} fusion(f32[640,16384]{1,0:T(8,128)} %get-tuple-element.48, f32[640]{0:T(1024)S(1)} %sub.53), kind=kLoop, calls=%fused_computation.3 | loop fusion | flops 20970880 | bytes 41948160 | tf_op jit(solution)/shard_map/reduce_sum | solution.py:93
  194.7 36.0 %all-reduce.12.cloned.1.call-done = f32[1,16384]{1,0:T(1,128)} async-done(((f32[1,16384]{1,0:T(1,128)}), f32[1,16384]{1,0:T(1,128)}) %all-reduce.12.cloned.1.call-update) | async-done | bytes 65552 | tf_op jit(solution)/shard_map/psum | solution.py:80
  236.6 11.7 %psum.116 = f32[128,1]{0,1:T(1,128)S(1)} all-reduce(f32[128,1]{0,1:T(1,128)S(1)} %bitcast.65), channel_id=1, replica_groups=mesh['vp'=4,'dp'=8] {'vp'}, use_global_device_ids=true, to_apply=%region_11.0 | all-reduce | flops 128 | bytes 1024 | tf_op jit(solution)/shard_map/psum | solution.py:82
  253.6 37.8 %reshape.68 = f32[64,10,16384]{2,1,0:T(8,128)} reshape(f32[640,16384]{1,0:T(8,128)} %get-tuple-element.48) | data formatting | bytes 83886080 | tf_op jit(solution)/shard_map/reshape | solution.py:89
  291.6 11.8 %all-reduce.14.cloned.1.call-done = f32[1,16384]{1,0:T(1,128)} async-done(((f32[1,16384]{1,0:T(1,128)}), f32[1,16384]{1,0:T(1,128)}) %all-reduce.14.cloned.1.call-update) | async-done | bytes 65552 | tf_op jit(solution)/shard_map/psum | solution.py:80
  308.9 19.5 %all-reduce.3 = (f32[128,1]{0,1:T(1,128)S(1)}, f32[64,10,1]{1,0,2:T(8,128)S(1)}) all-reduce(f32[128,1]{0,1:T(1,128)S(1)} %bitcast.63, f32[64,10,1]{1,0,2:T(8,128)S(1)} %broadcast_in_dim.44), channel_id=1, replica_groups=mesh['vp'=4,'dp'=8] {'vp'}, use_global_device_ids=true, to_apply=%region_15.0 | all-reduce | flops 768 | bytes 6144 | tf_op jit(solution)/shard_map/psum | solution.py:82
  328.4 6.8 fusion.17
  335.2 10.5 %reshape.67 = f32[64,2,16384]{2,1,0:T(2,128)} reshape(f32[128,16384]{1,0:T(8,128)} %fusion.17) | data formatting | bytes 16777216 | tf_op jit(solution)/shard_map/reshape | solution.py:84
  345.8 13.3 %reduce_sum.180 = f32[64,16384]{1,0:T(8,128)} reduce(f32[64,2,16384]{2,1,0:T(2,128)} %reshape.67, f32[]{:T(128)} %constant.50.clone.1), dimensions={1}, to_apply=%region_16.0 | reduce | flops 1048576 | bytes 12582916 | tf_op jit(solution)/shard_map/reduce_sum | solution.py:57
  359.1 39.1 %multiply_convert_fusion = (bf16[64,10,16384]{2,1,0:T(8,128)(2,1)}, f32[]{:T(128)}) fusion(f32[64,2,16384]{2,1,0:T(2,128)} %reshape.67, f32[64,10,16384]{2,1,0:T(8,128)} %reshape.68, f32[64,10]{1,0:T(8,128)S(1)} %bitcast.62, f32[10]{0:T(128)S(1)} %fusion.117, f32[64,10]{1,0:T(8,128)S(1)} %bitcast.58, f32[64,16384]{1,0:T(8,128)} %reduce_sum.180, ...), kind=kLoop, calls=%fused_computation | loop fusion | flops 104857600 | bytes 75505200 | tf_op jit(solution)/shard_map/convert_element_type | solution.py:98
  398.2 25.4 %convert_element_type.110 = bf16[640,16384]{1,0:T(8,128)(2,1)} reshape(bf16[64,10,16384]{2,1,0:T(8,128)(2,1)} %get-tuple-element.33) | data formatting | bytes 41943040 | tf_op jit(solution)/shard_map/convert_element_type | solution.py:98
  423.5 17.2 %fusion.114 = f32[256,16384]{1,0:T(8,128)} fusion(bf16[640,16384]{1,0:T(8,128)(2,1)} %convert_element_type.110, f32[640,256]{0,1:T(8,128)S(1)} %get-tuple-element.46, f32[640]{0:T(1024)S(1)} %rsqrt.34), kind=kOutput, calls=%fused_computation.176 | convolution fusion | flops 5369036800 | bytes 38406656 | tf_op jit(solution)/shard_map/rb,rk->bk/dot_general | solution.py:100
  441.1 21.9 %multiply_reduce_fusion.1 = (f32[640]{0:T(1024)S(1)}, f32[640,256]{0,1:T(8,128)S(1)}) fusion(f32[640,256]{0,1:T(8,128)S(1)} %get-tuple-element.46, f32[640]{0:T(1024)S(1)} %rsqrt.34, bf16[640,16384]{1,0:T(8,128)(2,1)} %convert_element_type.110, bf16[256,16384]{1,0:T(8,128)(2,1)} %param.24, f32[16384]{0:T(1024)S(1)} %rsqrt.35), kind=kOutput, calls=%fused_computation.138 | convolution fusion | flops 5381783040 | bytes 30741504 | tf_op jit(solution)/shard_map/rk,bk->rb/dot_general | solution.py:99
  470.4 9.2 fusion.150
  483.1 10.7 %fusion.58 = f32[2048,2048]{1,0:T(8,128)} fusion(bf16[640,2048]{1,0:T(8,128)(2,1)S(1)} %copy-done.23, bf16[640,2048]{1,0:T(8,128)(2,1)S(1)} %get-tuple-element.54), kind=kOutput, calls=%fused_computation.96 | convolution fusion | flops 5368709120 | bytes 22020096 | tf_op jit(solution)/shard_map/ng,nh->gh/dot_general | solution.py:37
  493.8 38.6 %all-reduce.1 = (f32[]{:T(128)}, f32[2048]{0:T(1024)}, f32[2048]{0:T(1024)}, f32[256]{0:T(256)}) all-reduce(f32[]{:T(128)} %get-tuple-element.34, f32[2048]{0:T(1024)S(1)} %get-tuple-element.51, f32[2048]{0:T(1024)S(1)} %get-tuple-element.53, f32[256]{0:T(256)S(1)} %get-tuple-element.35), channel_id=1, replica_groups=mesh['vp'=4,'dp'=8] {'vp','dp'}, use_global_device_ids=true, to_apply=%region_24.25 | all-reduce | flops 4353 | bytes 34824 | tf_op jit(solution)/shard_map/psum | solution.py:96
  533.0 123.3 %all-reduce.16.cloned.1.call-done = f32[256,16384]{1,0:T(8,128)} async-done(((f32[256,16384]{1,0:T(8,128)}), f32[256,16384]{1,0:T(8,128)}) %all-reduce.16.cloned.1.call-update) | async-done | bytes 16777232 | tf_op jit(solution)/shard_map/psum | solution.py:100
  656.3 9.2 fusion.6
  669.3 10.7 %fusion.8 = f32[256,16384]{1,0:T(8,128)} fusion(f32[256,16384]{1,0:T(8,128)S(1)} %copy-done.2, bf16[256,16384]{1,0:T(8,128)(2,1)} %param.24, f32[16384]{0:T(1024)S(1)} %fusion.6, f32[16384]{0:T(1024)S(1)} %rsqrt.35), kind=kLoop, calls=%fused_computation.18 | loop fusion | flops 20971520 | bytes 42074112 | tf_op jit(solution)/shard_map/mul | solution.py:52
  680.0 335.3 %all-reduce.18.cloned.1.call-done = (f32[384,2048]{0,1:T(8,128)}, f32[2048,2048]{1,0:T(8,128)}, f32[2048,256]{1,0:T(8,128)}) async-done(((f32[384,2048]{0,1:T(8,128)}, f32[2048,2048]{1,0:T(8,128)}, f32[2048,256]{1,0:T(8,128)}), (f32[384,2048]{0,1:T(8,128)}, f32[2048,2048]{1,0:T(8,128)}, f32[2048,256]{1,0:T(8,128)})) %all-reduce.18.cloned.1.call-update) | async-done | bytes 22020112 | tf_op jit(solution)/shard_map/psum | solution.py:101
  1018.9 12.7 %copy.38 = f32[2048,2048]{1,0:T(8,128)} copy(f32[2048,2048]{1,0:T(8,128)} %get-tuple-element.62) | data formatting | bytes 33554432
  (103 shorter events, 50.1 us)
Async XLA Ops:
  7.2 79.5 %copy-start = (bf16[384,2048]{1,0:T(8,128)(2,1)S(1)}, bf16[384,2048]{1,0:T(8,128)(2,1)}, u32[]{:S(2)}) copy-start(bf16[384,2048]{1,0:T(8,128)(2,1)} %param.18) | copy-start | bytes 4718596
  7.2 5.3 copy-start.20
  7.2 5.4 copy-start.11
  7.2 5.4 copy-start.12
  7.2 5.4 copy-start.19
  7.2 151.9 %all-reduce.10.cloned.1.call-start = ((), (), s32[]{:S(2)}) async-start(), calls=%async_computation | async-start | bytes 131072 | tf_op jit(solution)/shard_map/psum | solution.py:80
  12.6 10.1 copy-start.6
  81.2 5.4 copy-start.21
  81.2 5.4 copy-start.13
  81.2 5.4 copy-start.14
  81.2 5.5 copy-start.17
  81.2 149.6 %all-reduce.12.cloned.1.call-start = ((), (), s32[]{:S(2)}) async-start(), calls=%async_computation.1 | async-start | bytes 131072 | tf_op jit(solution)/shard_map/psum | solution.py:80
  81.3 19.2 %slice-start = ((s8[8388608]{0:T(1024)(128)(4,1)}), s8[4194304]{0:T(1024)(128)(4,1)S(1)}, s32[]{:S(2)}) async-start(s8[8388608]{0:T(1024)(128)(4,1)} %bitcast.66), calls=%async_computation.5 | async-start | bytes 8388608
  86.6 13.9 %copy-start.9 = (f32[2048]{0:T(1024)}, f32[2048]{0:T(1024)S(1)}, u32[]{:S(2)}) copy-start(f32[2048]{0:T(1024)S(1)} %convert_element_type.101) | copy-start | bytes 24580
  86.7 13.8 %copy-start.7 = (f32[2048]{0:T(1024)}, f32[2048]{0:T(1024)S(1)}, u32[]{:S(2)}) copy-start(f32[2048]{0:T(1024)S(1)} %convert_element_type.99) | copy-start | bytes 24580
  86.7 13.8 %slice-start.1 = ((s8[8388608]{0:T(1024)(128)(4,1)}), s8[4194304]{0:T(1024)(128)(4,1)S(1)}, s32[]{:S(2)}) async-start(s8[8388608]{0:T(1024)(128)(4,1)} %bitcast.66), calls=%async_computation.6 | async-start | bytes 8388608
  100.5 18.2 %copy-start.22 = (bf16[640,2048]{1,0:T(8,128)(2,1)}, bf16[640,2048]{1,0:T(8,128)(2,1)S(1)}, u32[]{:S(2)}) copy-start(bf16[640,2048]{1,0:T(8,128)(2,1)S(1)} %get-tuple-element.41) | copy-start | bytes 7864324
  100.5 19.7 %copy-start.15 = (bf16[2048,256]{1,0:T(8,128)(2,1)S(1)}, bf16[2048,256]{1,0:T(8,128)(2,1)}, u32[]{:S(2)}) copy-start(bf16[2048,256]{1,0:T(8,128)(2,1)} %param.22) | copy-start | bytes 3145732
  177.9 125.5 %all-reduce.14.cloned.1.call-start = ((), (), s32[]{:S(2)}) async-start(), calls=%async_computation.2 | async-start | bytes 131072 | tf_op jit(solution)/shard_map/psum | solution.py:80
  253.6 402.7 %all-reduce.16.cloned.1.call-start = ((), (), s32[]{:S(2)}) async-start(), calls=%async_computation.3 | async-start | bytes 33554432 | tf_op jit(solution)/shard_map/psum | solution.py:100
  440.8 574.5 %all-reduce.18.cloned.1.call-start = ((), (), s32[]{:S(2)}) async-start(), calls=%async_computation.4 | async-start | bytes 44040192 | tf_op jit(solution)/shard_map/psum | solution.py:101
  441.1 22.2 %copy-start.4 = (bf16[640,2048]{1,0:T(8,128)(2,1)S(1)}, bf16[640,2048]{1,0:T(8,128)(2,1)}, u32[]{:S(2)}) copy-start(bf16[640,2048]{1,0:T(8,128)(2,1)} %copy-done.3) | copy-start | bytes 7864324
  463.0 2.7 copy-start.10
  463.0 2.7 copy-start.16
  463.3 7.1 slice-start.2
  465.7 4.7 copy-start.8
  465.7 4.7 slice-start.3
  470.4 9.3 copy-start.18
  479.7 3.4 copy-start.23
  656.3 13.0 %copy-start.2 = (f32[256,16384]{1,0:T(8,128)S(1)}, f32[256,16384]{1,0:T(8,128)}, u32[]{:S(2)}) copy-start(f32[256,16384]{1,0:T(8,128)} %all-reduce.16.cloned.1.call-done) | copy-start | bytes 50331652
  1018.9 12.7 %copy-start.5 = (f32[2048,256]{1,0:T(8,128)S(1)}, f32[2048,256]{1,0:T(8,128)}, u32[]{:S(2)}) copy-start(f32[2048,256]{1,0:T(8,128)} %get-tuple-element.64) | copy-start | bytes 6291460
  1018.9 14.1 %copy-start.1 = (bf16[384,2048]{1,0:T(8,128)(2,1)S(1)}, bf16[384,2048]{1,0:T(8,128)(2,1)}, u32[]{:S(2)}) copy-start(bf16[384,2048]{1,0:T(8,128)(2,1)} %param.18) | copy-start | bytes 4718596
  (1 other events, 1.5 us)
Sparse Core Ops, SparseCore 0:
  81.4 53.0 all-reduce.9
  178.0 52.7 all-reduce.11
  253.7 49.6 all-reduce.13
  440.9 215.3 all-reduce.15
  663.1 352.1 all-reduce.17
where the time goes:
time: 1050 us; the launch traced here: 1040 us
  waiting for transfers between devices  507 us (48%)
  matrix products  142 us (14%)
  other arithmetic  139 us (13%)
  blocking collectives  139 us (13%)
  local copies, waits for them, and re-layouts  97.2 us (9%)
  between operations  17.2 us (2%)
    psum x1, waiting for transfers between devices, local_step(): lax.psum(mlp_backward(g_emb, student_x, saved, w_mid, w_out), ('vp', 'dp'))  335 us
    psum x1, waiting for transfers between devices, local_step(): lax.psum(jnp.einsum('rb,rk->bk', s_emb, g_logits, preferred_element_type=...  123 us
    psum x3, waiting for transfers between devices, local_step(): proto_sum = lax.psum(jnp.sum(q_mat, axis=0, keepdims=True), 'dp')  47.9 us
    psum x1, blocking collectives, local_step(): q_mat = q_mat / lax.psum(jnp.sum(q_mat), ('vp', 'dp'))  42.3 us
    psum x3, blocking collectives, local_step(): crop_sum = lax.psum(jnp.sum(q_mat, axis=1, keepdims=True), 'vp')  39.6 us
    convert_element_type x1, other arithmetic, local_step(): g_logits.reshape(n_img * ALL_CROPS, local_proto).astype(jnp.bfloat16)  39.1 us
    psum x1, blocking collectives, local_step(): lax.psum(jnp.sum(targets * (jnp.log(row_sum) - shifted)), ('vp', 'dp'))  38.6 us
    reshape x1, local copies, waits for them, and re-layouts, local_step(): logits = logits.reshape(n_img, ALL_CROPS, local_proto)  37.8 us
  transfers between devices with their start and end apart: 5, of which 4 were waited for; matrix products, arithmetic and copies ran while one was open for 18% of the time, Pallas kernels for 0%

commit v1 on v0

v1 whole, which is shorter than its diff:
```python
import jax
import jax.numpy as jnp
from jax import lax
from jax.sharding import PartitionSpec as P

ALL_CROPS = 10
GLOBAL_CROPS = 2
SINK_ITERS = 3
TEMP_STUDENT = 0.1
TEMP_TEACHER = 0.04
F32 = jnp.float32
BF16 = jnp.bfloat16


def gelu_slope(pre):
    cdf = 0.5 * (1.0 + lax.erf(pre * 0.7071067811865476))
    return cdf + pre * jnp.exp(-0.5 * pre * pre) * 0.3989422804014327


def mlp_forward(feats, w_in, b_in, w_mid, b_mid, w_out, b_out):
    pre_one = jnp.dot(feats, w_in, preferred_element_type=F32) + b_in.astype(F32)
    hid_one = jax.nn.gelu(pre_one, approximate=False).astype(BF16)
    pre_two = jnp.dot(hid_one, w_mid, preferred_element_type=F32) + b_mid.astype(F32)
    hid_two = jax.nn.gelu(pre_two, approximate=False).astype(BF16)
    proj = jnp.dot(hid_two, w_out, preferred_element_type=F32) + b_out.astype(F32)
    inv_norm = lax.rsqrt(jnp.sum(proj * proj, axis=-1, keepdims=True))
    unit = proj * inv_norm
    return unit.astype(BF16), proj, (pre_one, hid_one, pre_two, hid_two, unit, inv_norm)


def col_normalize(protos):
    proto_f = protos.astype(F32)
    inv_col = lax.rsqrt(jnp.sum(proto_f * proto_f, axis=0, keepdims=True))
    unit = proto_f * inv_col
    return unit.astype(BF16), unit, inv_col


def pair_targets(q_three):
    pad_rows = ALL_CROPS - GLOBAL_CROPS
    return jnp.sum(q_three, axis=1, keepdims=True) - jnp.pad(q_three, ((0, 0), (0, pad_rows), (0, 0)))


def crop_counts():
    crop_idx = jnp.arange(ALL_CROPS)
    return (GLOBAL_CROPS - (crop_idx < GLOBAL_CROPS).astype(jnp.int32)).astype(F32)


def solution(mesh):
    vp_size = mesh.shape['vp']
    dp_size = mesh.shape['dp']

    def local_step(student_x, teacher_x, w_in, b_in, w_mid, b_mid, w_out, b_out, protos,
                   ema_w_in, ema_b_in, ema_w_mid, ema_b_mid, ema_w_out, ema_b_out, ema_protos):
        n_img = student_x.shape[0] // ALL_CROPS
        local_proto = protos.shape[1]
        n_proto = local_proto * vp_size
        n_rows = GLOBAL_CROPS * n_img * dp_size
        hidden = w_mid.shape[0]
        bott = w_out.shape[1]
        in_dim = w_in.shape[0]
        i_dp = lax.axis_index('dp')
        i_vp = lax.axis_index('vp')
        scale = 1.0 / (n_img * dp_size * GLOBAL_CROPS * (ALL_CROPS - 1))

        t_emb, t_proj, _ = mlp_forward(teacher_x, ema_w_in, ema_b_in, ema_w_mid, ema_b_mid, ema_w_out, ema_b_out)
        t_unit = col_normalize(ema_protos)[0]
        e_mat = jnp.exp(jnp.dot(t_emb, t_unit, preferred_element_type=F32) / TEMP_TEACHER)
        col_raw = lax.psum(jnp.sum(e_mat, axis=0, keepdims=True), 'dp')

        s_emb, s_proj, saved = mlp_forward(student_x, w_in, b_in, w_mid, b_mid, w_out, b_out)
        s_unit = col_normalize(protos)[0]
        emb_all = lax.all_gather(jnp.concatenate([s_proj, t_proj], axis=0), 'dp', axis=0)
        emb_all = emb_all * lax.rsqrt(jnp.sum(emb_all * emb_all, axis=-1, keepdims=True))
        logits = jnp.dot(s_emb, s_unit, preferred_element_type=F32) / TEMP_STUDENT
        exp_s = jnp.exp(logits)
        srow = jnp.sum(exp_s, axis=-1, keepdims=True)

        b_raw = 1.0 / (col_raw * n_proto)
        rows = jnp.sum(e_mat * b_raw, axis=1, keepdims=True)
        tot = jnp.sum(col_raw).reshape(1, 1)
        packed = lax.psum(jnp.concatenate([rows, srow, tot], axis=0), 'vp')
        nt = rows.shape[0]
        total = packed[-1:, :]
        row_sum = packed[nt:-1, :]
        inv_total = 1.0 / total
        a_vec = inv_total / ((packed[:nt, :] * (inv_total * total)) * n_rows)
        b_vec = b_raw * total
        for _ in range(SINK_ITERS - 1):
            col = lax.psum(jnp.sum(e_mat * a_vec, axis=0, keepdims=True), 'dp')
            b_vec = 1.0 / (col * n_proto)
            row = lax.psum(jnp.sum(e_mat * b_vec, axis=1, keepdims=True), 'vp')
            a_vec = 1.0 / (row * n_rows)
        a_fin = a_vec * n_rows

        def grad_logits(logit, e_blk, a_col, b_row, rsum):
            nr = logit.shape[0]
            kk = logit.shape[1]
            q_three = (e_blk * a_col * b_row).reshape(nr // ALL_CROPS, GLOBAL_CROPS, kk)
            targets = pair_targets(q_three)
            prob = (jnp.exp(logit) / rsum).reshape(nr // ALL_CROPS, ALL_CROPS, kk)
            g = (crop_counts()[:, None] * prob - targets) * (scale / TEMP_STUDENT)
            return g.reshape(nr, kk).astype(BF16), targets

        g_logits, targets = grad_logits(logits, e_mat, a_fin, b_vec, row_sum)
        lg3 = logits.reshape(targets.shape)
        loss_part = jnp.sum(targets * (jnp.log(row_sum).reshape(n_img, ALL_CROPS, 1) - lg3)) * scale
        g_emb = lax.psum(jnp.einsum('rk,bk->rb', g_logits, s_unit, preferred_element_type=F32), 'vp')

        own = local_proto // dp_size
        c0 = i_dp * own
        small = lax.all_gather(jnp.concatenate([row_sum, a_fin], axis=0), 'dp', axis=0)
        n_s = s_emb.shape[0]
        s_all = emb_all[:, :n_s].reshape(-1, bott).astype(BF16)
        t_all = emb_all[:, n_s:].reshape(-1, bott).astype(BF16)
        rs_all = small[:, :n_s].reshape(-1, 1)
        a_all = small[:, n_s:].reshape(-1, 1)
        p_own = lax.dynamic_slice_in_dim(protos, c0, own, axis=1)
        su_own, su_f, inv_own = col_normalize(p_own)
        tu_own = col_normalize(lax.dynamic_slice_in_dim(ema_protos, c0, own, axis=1))[0]
        b_own = lax.dynamic_slice_in_dim(b_vec, c0, own, axis=1)
        lg_own = jnp.dot(s_all, su_own, preferred_element_type=F32) / TEMP_STUDENT
        e_own = jnp.exp(jnp.dot(t_all, tu_own, preferred_element_type=F32) / TEMP_TEACHER)
        gl_own, _ = grad_logits(lg_own, e_own, a_all, b_own, rs_all)
        gu = jnp.einsum('rb,rk->bk', s_all, gl_own, preferred_element_type=F32)
        gp_own = (gu - su_f * jnp.sum(su_f * gu, axis=0, keepdims=True)) * inv_own
        g_protos = lax.all_gather(gp_own, 'dp', axis=1, tiled=True)

        pre_one, hid_one, pre_two, hid_two, unit, inv_norm = saved
        qh = hidden // vp_size
        h0 = i_vp * qh
        g_proj = (g_emb - unit * jnp.sum(unit * g_emb, axis=-1, keepdims=True)) * inv_norm
        g_proj_lo = g_proj.astype(BF16)
        g_hid_two = jnp.einsum('nb,hb->nh', g_proj_lo, w_out, preferred_element_type=F32)
        g_pre_two = g_hid_two * gelu_slope(pre_two)
        g_pre_two_lo = g_pre_two.astype(BF16)
        hid_two_q = lax.dynamic_slice_in_dim(hid_two, h0, qh, axis=1)
        hid_one_q = lax.dynamic_slice_in_dim(hid_one, h0, qh, axis=1)
        pre_one_q = lax.dynamic_slice_in_dim(pre_one, h0, qh, axis=1)
        w_mid_q = lax.dynamic_slice_in_dim(w_mid, h0, qh, axis=0)
        g_w_out_q = jnp.einsum('nh,nb->hb', hid_two_q, g_proj_lo, preferred_element_type=F32)
        g_w_mid_q = jnp.einsum('ng,nh->gh', hid_one_q, g_pre_two_lo, preferred_element_type=F32)
        g_hid_one_q = jnp.einsum('nh,gh->ng', g_pre_two_lo, w_mid_q, preferred_element_type=F32)
        g_pre_one_q = g_hid_one_q * gelu_slope(pre_one_q)
        g_w_in_q = jnp.einsum('nh,nf->hf', g_pre_one_q.astype(BF16), student_x, preferred_element_type=F32)
        bq = bott // vp_size
        gb_in = jnp.sum(g_pre_one_q, axis=0)
        gb_mid = lax.dynamic_slice_in_dim(jnp.sum(g_pre_two, axis=0), h0, qh, axis=0)
        gb_out = lax.dynamic_slice_in_dim(jnp.sum(g_proj, axis=0), i_vp * bq, bq, axis=0)
        tail = jnp.stack([gb_in, gb_mid, jnp.pad(gb_out, (0, qh - bq)),
                          jnp.pad(loss_part.reshape(1), (0, qh - 1))], axis=1)
        stack = jnp.concatenate([g_w_mid_q, g_w_in_q, g_w_out_q, jnp.pad(tail, ((0, 0), (0, 124)))], axis=1)
        part = lax.psum_scatter(stack, 'dp', scatter_dimension=0, tiled=True)
        full = lax.all_gather(part, ('vp', 'dp'), axis=0, tiled=True)
        e1 = hidden
        e2 = e1 + in_dim
        e3 = e2 + bott
        tails = full[:, e3:]
        loss = jnp.sum(tails.reshape(vp_size, qh, 128)[:, 0, 3])
        o_b_out = tails.reshape(vp_size, qh, 128)[:, :bq, 2].reshape(bott)
        return (loss, full[:, e1:e2].T, tails[:, 0], full[:, :e1], tails[:, 1], full[:, e2:e3], o_b_out, g_protos)

    by_rows = P('dp', None)
    by_cols = P(None, 'vp')
    replicated = P()
    head_specs = (replicated,) * 6
    in_specs = (by_rows, by_rows) + head_specs + (by_cols,) + head_specs + (by_cols,)
    out_specs = (replicated,) * 7 + (by_cols,)
    return jax.shard_map(local_step, mesh=mesh, in_specs=in_specs, out_specs=out_specs, check_vma=False)
```

time: 1050 us -> 1010 us (0.962)
  waiting for transfers between devices: 507 us -> 339 us
  local copies, waits for them, and re-layouts: 97.2 us -> 244 us
  blocking collectives: 139 us -> 51.5 us
  other arithmetic: 139 us -> 212 us
    psum x5 -> x4, waiting for transfers between devices: 506 us -> 76.5 us  [the longest x2 50.8 us: local_step(): col = lax.psum(jnp.sum(e_mat * a_vec, axis=0, keepdims=True), 'dp')]
    all_gather x0 -> x3, waiting for transfers between devices: none -> 261 us  [the longest x1 146 us: local_step(): full = lax.all_gather(part, ('vp', 'dp'), axis=0, tiled=True)]
    reshape x2 -> x5, local copies, waits for them, and re-layouts: 48.4 us -> 144 us  [the longest x2 85 us: grad_logits(): prob = (jnp.exp(logit) / rsum).reshape(nr // ALL_CROPS, ALL_CROPS, kk)]
    psum x5 -> x3, blocking collectives: 121 us -> 42.9 us  [the longest x1 22.9 us: local_step(): packed = lax.psum(jnp.concatenate([rows, srow, tot], axis=0), 'vp')]
    convert_element_type x8 -> x9, other arithmetic: 39.2 us -> 94.7 us  [the longest x2 94.6 us: grad_logits(): return (g.reshape(nr, kk).astype(BF16), targets)]
    convert_element_type x1 -> x2, local copies, waits for them, and re-layouts: 25.4 us -> 60.2 us  [grad_logits(): return (g.reshape(nr, kk).astype(BF16), targets)]
    div x3 -> x4, other arithmetic: 0.02 us -> 32.5 us  [the longest x1 29.1 us: grad_logits(): prob = (jnp.exp(logit) / rsum).reshape(nr // ALL_CROPS, ALL_CROPS, kk)]
    reduce_sum x9, other arithmetic: 55.8 us -> 28.8 us  [the longest x2 9.54 us: local_step(): col = lax.psum(jnp.sum(e_mat * a_vec, axis=0, keepdims=True), 'dp')]
  transfers between devices with their start and end apart: 5 -> 8, of which waited for: 4 -> 5; matrix products, arithmetic and copies ran while one was open for 18% -> 37% of each run, Pallas kernels for 0% -> 0%
where the time goes in v1:
time: 1010 us; the launch traced here: 1000 us
  waiting for transfers between devices  339 us (34%)
  local copies, waits for them, and re-layouts  244 us (24%)
  other arithmetic  212 us (21%)
  matrix products  137 us (14%)
  blocking collectives  51.5 us (5%)
  between operations  17.2 us (2%)
    all_gather x1, waiting for transfers between devices, local_step(): full = lax.all_gather(part, ('vp', 'dp'), axis=0, tiled=True)  146 us
    convert_element_type x2, other arithmetic, grad_logits(): return (g.reshape(nr, kk).astype(BF16), targets)  94.6 us
    all_gather x1, waiting for transfers between devices, local_step(): g_protos = lax.all_gather(gp_own, 'dp', axis=1, tiled=True)  89 us
    reshape x2, local copies, waits for them, and re-layouts, grad_logits(): prob = (jnp.exp(logit) / rsum).reshape(nr // ALL_CROPS, ALL_CROPS, kk)  85 us
    convert_element_type x2, local copies, waits for them, and re-layouts, grad_logits(): return (g.reshape(nr, kk).astype(BF16), targets)  60.2 us
    psum x2, waiting for transfers between devices, local_step(): col = lax.psum(jnp.sum(e_mat * a_vec, axis=0, keepdims=True), 'dp')  50.8 us
    reshape x1, local copies, waits for them, and re-layouts, local_step(): lg3 = logits.reshape(targets.shape)  37.8 us
    div x1, other arithmetic, grad_logits(): prob = (jnp.exp(logit) / rsum).reshape(nr // ALL_CROPS, ALL_CROPS, kk)  29.1 us
  transfers between devices with their start and end apart: 8, of which 5 were waited for; matrix products, arithmetic and copies ran while one was open for 37% of the time, Pallas kernels for 0%

profile of v1, /device:TPU:0, one launch (start us, length us, event | category | flops | bytes accessed | tf_op | source)
XLA Modules:
  0.0 1000.6 jit_solution(14485554871116697272)
XLA Ops:
  12.6 10.1 %fusion.61 = bf16[128,2048]{1,0:T(8,128)(2,1)S(1)} fusion(bf16[2048,2048]{1,0:T(8,128)(2,1)} %param.27, bf16[128,384]{1,0:T(8,128)(2,1)S(1)} %copy-done.30, bf16[384,2048]{1,0:T(8,128)(2,1)} %param.25, f32[2048]{0:T(1024)S(1)} %convert_element_type.134, f32[2048]{0:T(1024)S(1)} %convert_element_type.132), kind=kOutput, calls=%fused_computation.113 | convolution fusion | flops 1309671424 | bytes 10600448 | tf_op jit(solution)/shard_map/dot_general | solution.py:23
  23.1 10.6 %fusion.163 = (f32[16384]{0:T(1024)}, f32[128,16384]{1,0:T(8,128)}) fusion(bf16[256,16384]{1,0:T(8,128)(2,1)} %param.31, f32[16384]{0:T(1024)S(1)} %rsqrt.59, f32[128,256]{1,0:T(8,128)S(1)} %get-tuple-element.52, f32[128]{0:T(128)S(1)} %rsqrt.58), kind=kOutput, calls=%fused_computation.255 | convolution fusion | flops 1090568192 | bytes 17039872 | tf_op jit(solution)/shard_map/dot_general | solution.py:67
  39.5 13.8 %fusion.12 = (bf16[640,2048]{1,0:T(8,128)(2,1)S(1)}, f32[640,2048]{1,0:T(8,128)}) fusion(f32[2048]{0:T(1024)S(1)} %convert_element_type.122, bf16[640,384]{1,0:T(8,128)(2,1)S(1)} %copy-done.13, bf16[384,2048]{1,0:T(8,128)(2,1)S(1)} %copy-done), kind=kOutput, calls=%fused_computation.35 | convolution fusion | flops 1093140480 | bytes 9936896 | tf_op jit(solution)/shard_map/dot_general | solution.py:21
  53.3 18.2 %fusion.15 = (bf16[640,2048]{1,0:T(8,128)(2,1)S(1)}, f32[640,2048]{1,0:T(8,128)}) fusion(f32[2048]{0:T(1024)S(1)} %convert_element_type.126, bf16[640,2048]{1,0:T(8,128)(2,1)S(1)} %get-tuple-element.55, bf16[2048,2048]{1,0:T(8,128)(2,1)S(1)} %bitcast.91), kind=kOutput, calls=%fused_computation.38 | convolution fusion | flops 5455216640 | bytes 18882560 | tf_op jit(solution)/shard_map/dot_general | solution.py:23
  73.0 19.9 %exponential_reduce_fusion = (f32[640]{0:T(1024)S(1)}, f32[640,16384]{1,0:T(8,128)}) fusion(bf16[256,16384]{1,0:T(8,128)(2,1)} %param.24, f32[16384]{0:T(1024)S(1)} %rsqrt.57, f32[640,256]{1,0:T(8,128)S(1)} %get-tuple-element.60, f32[640]{0:T(1024)S(1)} %rsqrt.56), kind=kOutput, calls=%fused_computation.6 | convolution fusion | flops 5402590720 | bytes 51057664 | tf_op jit(solution)/shard_map/dot_general | solution.py:74
  92.9 37.8 %reshape.108 = f32[64,10,16384]{2,1,0:T(8,128)} reshape(f32[640,16384]{1,0:T(8,128)} %get-tuple-element.62) | data formatting | bytes 83886080 | tf_op jit(solution)/shard_map/reshape | solution.py:105
  137.0 22.9 %psum.50 = f32[769,1]{0,1:T(1,128)S(1)} all-reduce(f32[769,1]{0,1:T(1,128)S(1)} %pad_maximum_fusion.2), channel_id=1, replica_groups=mesh['vp'=4,'dp'=8] {'vp'}, use_global_device_ids=true, to_apply=%region_9.0 | all-reduce | flops 769 | bytes 6152 | tf_op jit(solution)/shard_map/psum | solution.py:81
  167.2 50.8 %all-reduce.12.cloned.1.call-done = f32[1,16384]{1,0:T(1,128)} async-done(((f32[1,16384]{1,0:T(1,128)}), f32[1,16384]{1,0:T(1,128)}) %all-reduce.12.cloned.1.call-update) | async-done | bytes 65552 | tf_op jit(solution)/shard_map/psum | solution.py:89
  222.9 11.7 %psum.52 = f32[128,1]{0,1:T(1,128)S(1)} all-reduce(f32[128,1]{0,1:T(1,128)S(1)} %bitcast.88), channel_id=1, replica_groups=mesh['vp'=4,'dp'=8] {'vp'}, use_global_device_ids=true, to_apply=%region_13.0 | all-reduce | flops 128 | bytes 1024 | tf_op jit(solution)/shard_map/psum | solution.py:91
  239.4 29.1 %exponential_divide_fusion.1 = f32[640,16384]{1,0:T(8,128)} fusion(f32[640,16384]{1,0:T(8,128)} %get-tuple-element.62, f32[640]{0:T(1024)S(1)} %get-tuple-element.42), kind=kLoop, calls=%fused_computation.5 | loop fusion | flops 10485760 | bytes 83888640 | tf_op jit(solution)/shard_map/div | solution.py:100
  268.5 37.5 %reshape.106 = f32[64,10,16384]{2,1,0:T(8,128)} reshape(f32[640,16384]{1,0:T(8,128)} %exponential_divide_fusion.1) | data formatting | bytes 83886080 | tf_op jit(solution)/shard_map/reshape | solution.py:100
  311.2 8.4 psum.54
  319.5 7.8 multiply_multiply_fusion.1
  327.3 10.5 %reshape.107 = f32[64,2,16384]{2,1,0:T(2,128)} reshape(f32[128,16384]{1,0:T(8,128)} %multiply_multiply_fusion.1) | data formatting | bytes 16777216 | tf_op jit(solution)/shard_map/reshape | solution.py:98
  337.8 13.3 %reduce_sum.228 = f32[64,16384]{1,0:T(8,128)} reduce(f32[64,2,16384]{2,1,0:T(2,128)} %reshape.107, f32[]{:T(128)} %constant.58.clone.1), dimensions={1}, to_apply=%region_18.0 | reduce | flops 1048576 | bytes 12582916 | tf_op jit(solution)/shard_map/reduce_sum | solution.py:40
  351.1 58.1 %multiply_convert_fusion.1 = (bf16[64,10,16384]{2,1,0:T(8,128)(2,1)}, f32[]{:T(128)}) fusion(f32[64,2,16384]{2,1,0:T(2,128)} %reshape.107, f32[64,10,16384]{2,1,0:T(8,128)} %reshape.106, f32[64,16384]{1,0:T(8,128)} %reduce_sum.228, f32[10]{0:T(128)S(1)} %fusion.128, f32[64,10,16384]{2,1,0:T(8,128)} %reshape.108, f32[64,10]{1,0:T(8,128)S(1)} %sub.53), kind=kLoop, calls=%fused_computation.2 | loop fusion | flops 83886080 | bytes 117443120 | tf_op jit(solution)/shard_map/convert_element_type | solution.py:102
  409.2 25.4 %convert_element_type.141 = bf16[640,16384]{1,0:T(8,128)(2,1)} reshape(bf16[64,10,16384]{2,1,0:T(8,128)(2,1)} %get-tuple-element.46) | data formatting | bytes 41943040 | tf_op jit(solution)/shard_map/convert_element_type | solution.py:102
  434.6 13.1 %fusion.7 = f32[640,256]{1,0:T(8,128)} fusion(bf16[640,16384]{1,0:T(8,128)(2,1)} %convert_element_type.141, bf16[256,16384]{1,0:T(8,128)(2,1)} %param.24, f32[16384]{0:T(1024)S(1)} %copy-done.16), kind=kOutput, calls=%fused_computation.29 | convolution fusion | flops 5381292032 | bytes 30081024 | tf_op jit(solution)/shard_map/rk,bk->rb/dot_general | solution.py:107
  452.5 8.6 all-gather.1
  461.1 25.7 %all-reduce.16.cloned.1.call-done = f32[640,256]{1,0:T(8,128)} async-done(((f32[640,256]{1,0:T(8,128)}), f32[640,256]{1,0:T(8,128)}) %all-reduce.16.cloned.1.call-update) | async-done | bytes 655376 | tf_op jit(solution)/shard_map/psum | solution.py:107
  507.7 26.0 %all-gather.10.cloned.1.call-done = f32[6144,256]{1,0:T(8,128)} async-done(((f32[768,256]{1,0:T(8,128)}), f32[6144,256]{1,0:T(8,128)}) %all-gather.10.cloned.1.call-update) | async-done | bytes 6291472 | tf_op jit(solution)/shard_map/all_gather | solution.py:72
  539.5 18.0 %exponential_divide_fusion = f32[5120,2048]{1,0:T(8,128)} fusion(bf16[5120,256]{1,0:T(8,128)(2,1)S(1)} %bitcast.67, f32[5120]{0:T(1024)S(1)} %div.90, f32[2048]{0:T(1024)S(1)} %rsqrt.61, bf16[256,16384]{1,0:T(8,128)(2,1)} %param.24, s32[]{:T(128)S(6)} %select_n.8), kind=kOutput, calls=%fused_computation.4 | convolution fusion | flops 5391253504 | bytes 45641732 | tf_op jit(solution)/shard_map/dot_general | solution.py:121
  557.5 6.4 multiply_multiply_fusion
  563.9 10.5 %reshape.112 = f32[512,2,2048]{2,1,0:T(2,128)} reshape(f32[1024,2048]{1,0:T(8,128)} %multiply_multiply_fusion) | data formatting | bytes 16777216 | tf_op jit(solution)/shard_map/reshape | solution.py:98
  574.5 47.4 %reshape.111 = f32[512,10,2048]{2,1,0:T(8,128)} reshape(f32[5120,2048]{1,0:T(8,128)} %exponential_divide_fusion) | data formatting | bytes 83886080 | tf_op jit(solution)/shard_map/reshape | solution.py:100
  621.9 13.3 %reduce_sum.238 = f32[512,2048]{1,0:T(8,128)} reduce(f32[512,2,2048]{2,1,0:T(2,128)} %reshape.112, f32[]{:T(128)} %constant.58.clone.1), dimensions={1}, to_apply=%region_30.31 | reduce | flops 1048576 | bytes 12582916 | tf_op jit(solution)/shard_map/reduce_sum | solution.py:40
  635.2 36.6 %multiply_convert_fusion = bf16[512,10,2048]{2,1,0:T(8,128)(2,1)} fusion(f32[512,2,2048]{2,1,0:T(2,128)} %reshape.112, f32[512,10,2048]{2,1,0:T(8,128)} %reshape.111, f32[512,2048]{1,0:T(8,128)} %reduce_sum.238, f32[10]{0:T(128)S(1)} %copy-done.27), kind=kLoop, calls=%fused_computation | loop fusion | flops 52428800 | bytes 75497512 | tf_op jit(solution)/shard_map/convert_element_type | solution.py:102
  671.8 34.9 %convert_element_type.153 = bf16[5120,2048]{1,0:T(8,128)(2,1)} reshape(bf16[512,10,2048]{2,1,0:T(8,128)(2,1)} %multiply_convert_fusion) | data formatting | bytes 41943040 | tf_op jit(solution)/shard_map/convert_element_type | solution.py:102
  706.6 10.8 %fusion.38 = (f32[2048]{0:T(1024)S(1)}, f32[256,2048]{1,0:T(8,128)S(1)}) fusion(f32[2048]{0:T(1024)S(1)} %rsqrt.61, bf16[256,16384]{1,0:T(8,128)(2,1)} %param.24, s32[]{:T(128)S(6)} %select_n.8, bf16[5120,256]{1,0:T(8,128)(2,1)} %bitcast.68, bf16[5120,2048]{1,0:T(8,128)(2,1)} %convert_element_type.153), kind=kOutput, calls=%fused_computation.87 | convolution fusion | flops 5370804224 | bytes 26755076 | tf_op jit(solution)/shard_map/rb,rk->bk/dot_general | solution.py:124
  721.2 89.0 %all-gather.8.cloned.1.call-done = f32[256,16384]{1,0:T(8,128)} async-done(((f32[256,2048]{1,0:T(8,128)}), f32[256,16384]{1,0:T(8,128)}) %all-gather.8.cloned.1.call-update) | async-done | bytes 16777232 | tf_op jit(solution)/shard_map/all_gather | solution.py:126
  810.3 146.2 %all-gather.6.cloned.1.call-done = f32[2048,2816]{1,0:T(8,128)} async-done(((f32[64,2816]{1,0:T(8,128)}), f32[2048,2816]{1,0:T(8,128)}) %all-gather.6.cloned.1.call-update) | async-done | bytes 23068688 | tf_op jit(solution)/shard_map/all_gather | solution.py:153
  969.8 13.6 %slice.70 = f32[2048,2048]{1,0:T(8,128)} slice(f32[2048,2816]{1,0:T(8,128)} %all-gather.6.cloned.1.call-done), slice={[0:2048], [0:2048]} | slice | bytes 33554432 | tf_op jit(solution)/shard_map/slice | solution.py:160
  (171 shorter events, 97.5 us)
Async XLA Ops:
  7.2 32.3 %copy-start = (bf16[384,2048]{1,0:T(8,128)(2,1)S(1)}, bf16[384,2048]{1,0:T(8,128)(2,1)}, u32[]{:S(2)}) copy-start(bf16[384,2048]{1,0:T(8,128)(2,1)} %param.18) | copy-start | bytes 4718596
  7.2 123.5 %all-reduce.10.cloned.1.call-start = ((), (), s32[]{:S(2)}) async-start(), calls=%async_computation.1 | async-start | bytes 131072 | tf_op jit(solution)/shard_map/psum | solution.py:68
  23.1 10.6 %copy-start.11 = (f32[128,256]{1,0:T(8,128)}, f32[128,256]{1,0:T(8,128)S(1)}, u32[]{:S(2)}) copy-start(f32[128,256]{1,0:T(8,128)S(1)} %get-tuple-element.52) | copy-start | bytes 393220
  33.8 184.2 %all-reduce.12.cloned.1.call-start = ((), (), s32[]{:S(2)}) async-start(), calls=%async_computation.2 | async-start | bytes 131072 | tf_op jit(solution)/shard_map/psum | solution.py:89
  34.1 19.2 %slice-start.4 = ((s8[8388608]{0:T(1024)(128)(4,1)}), s8[4194304]{0:T(1024)(128)(4,1)S(1)}, s32[]{:S(2)}) async-start(s8[8388608]{0:T(1024)(128)(4,1)} %bitcast.90), calls=%async_computation.13 | async-start | bytes 8388608
  39.4 33.6 %copy-start.15 = (f32[16384]{0:T(1024)}, f32[16384]{0:T(1024)S(1)}, u32[]{:S(2)}) copy-start(f32[16384]{0:T(1024)S(1)} %rsqrt.57) | copy-start | bytes 196612
  39.5 13.9 %copy-start.20 = (f32[2048]{0:T(1024)}, f32[2048]{0:T(1024)S(1)}, u32[]{:S(2)}) copy-start(f32[2048]{0:T(1024)S(1)} %convert_element_type.126) | copy-start | bytes 24580
  39.5 13.8 %slice-start.5 = ((s8[8388608]{0:T(1024)(128)(4,1)}), s8[4194304]{0:T(1024)(128)(4,1)S(1)}, s32[]{:S(2)}) async-start(s8[8388608]{0:T(1024)(128)(4,1)} %bitcast.90), calls=%async_computation.14 | async-start | bytes 8388608
  53.3 18.2 %copy-start.18 = (bf16[640,2048]{1,0:T(8,128)(2,1)}, bf16[640,2048]{1,0:T(8,128)(2,1)S(1)}, u32[]{:S(2)}) copy-start(bf16[640,2048]{1,0:T(8,128)(2,1)S(1)} %get-tuple-element.55) | copy-start | bytes 7864324
  53.3 18.2 %copy-start.28 = (bf16[2048,256]{1,0:T(8,128)(2,1)S(1)}, bf16[2048,256]{1,0:T(8,128)(2,1)}, u32[]{:S(2)}) copy-start(bf16[2048,256]{1,0:T(8,128)(2,1)} %param.22) | copy-start | bytes 3145732
  73.0 19.9 %copy-start.4 = (f32[640,256]{1,0:T(8,128)}, f32[640,256]{1,0:T(8,128)S(1)}, u32[]{:S(2)}) copy-start(f32[640,256]{1,0:T(8,128)S(1)} %get-tuple-element.60) | copy-start | bytes 1966084
  73.0 19.9 %copy-start.9 = (f32[640]{0:T(1024)}, f32[640]{0:T(1024)S(1)}, u32[]{:S(2)}) copy-start(f32[640]{0:T(1024)S(1)} %rsqrt.56) | copy-start | bytes 7684
  92.9 258.2 %copy-start.26 = (f32[10]{0:T(128)}, f32[10]{0:T(128)S(1)}, u32[]{:S(2)}) copy-start(f32[10]{0:T(128)S(1)} %fusion.128) | copy-start | bytes 124
  166.6 139.6 %all-reduce.14.cloned.1.call-start = ((), (), s32[]{:S(2)}) async-start(), calls=%async_computation.3 | async-start | bytes 131072 | tf_op jit(solution)/shard_map/psum | solution.py:89
  239.4 247.4 %all-reduce.16.cloned.1.call-start = ((), (), s32[]{:S(2)}) async-start(), calls=%async_computation.4 | async-start | bytes 1310720 | tf_op jit(solution)/shard_map/psum | solution.py:107
  409.2 25.4 %copy-start.16 = (f32[16384]{0:T(1024)S(1)}, f32[16384]{0:T(1024)}, u32[]{:S(2)}) copy-start(f32[16384]{0:T(1024)} %copy-done.15) | copy-start | bytes 196612
  434.6 13.2 %copy-start.5 = (f32[640,256]{1,0:T(8,128)S(1)}, f32[640,256]{1,0:T(8,128)}, u32[]{:S(2)}) copy-start(f32[640,256]{1,0:T(8,128)} %copy-done.4) | copy-start | bytes 1966084
  434.6 13.2 %copy-start.12 = (f32[128,256]{1,0:T(8,128)S(1)}, f32[128,256]{1,0:T(8,128)}, u32[]{:S(2)}) copy-start(f32[128,256]{1,0:T(8,128)} %copy-done.11) | copy-start | bytes 393220
  434.6 17.8 %copy-start.19 = (f32[640,1]{0,1:T(1,128)S(1)}, f32[640,1]{0,1:T(1,128)}, u32[]{:S(2)}) copy-start(f32[640,1]{0,1:T(1,128)} %get-tuple-element.50) | copy-start | bytes 7684
  447.7 39.0 %copy-start.10 = (f32[640]{0:T(1024)S(1)}, f32[640]{0:T(1024)}, u32[]{:S(2)}) copy-start(f32[640]{0:T(1024)} %copy-done.9) | copy-start | bytes 7684
  447.7 41.8 %copy-start.21 = (f32[2048]{0:T(1024)S(1)}, f32[2048]{0:T(1024)}, u32[]{:S(2)}) copy-start(f32[2048]{0:T(1024)} %copy-done.20) | copy-start | bytes 24580
  447.7 41.8 %copy-start.29 = (bf16[2048,256]{1,0:T(8,128)(2,1)S(1)}, bf16[2048,256]{1,0:T(8,128)(2,1)}, u32[]{:S(2)}) copy-start(bf16[2048,256]{1,0:T(8,128)(2,1)} %param.22) | copy-start | bytes 3145732
  447.8 86.0 %all-gather.10.cloned.1.call-start = ((), (), s32[]{:S(2)}) async-start(), calls=%async_computation.8 | async-start | bytes 7077888 | tf_op jit(solution)/shard_map/all_gather | solution.py:72
  448.8 271.8 %reduce-scatter.2.cloned.1.call-start = ((), (), s32[]{:S(2)}) async-start(), calls=%async_computation.5 | async-start | bytes 6488064 | tf_op jit(solution)/shard_map/reduce_scatter | solution.py:152
  507.6 302.7 %all-gather.8.cloned.1.call-start = ((), (), s32[]{:S(2)}) async-start(), calls=%async_computation.7 | async-start | bytes 18874368 | tf_op jit(solution)/shard_map/all_gather | solution.py:126
  539.5 18.0 %copy-start.3 = (bf16[8,640,256]{2,1,0:T(8,128)(2,1)}, bf16[8,640,256]{2,1,0:T(8,128)(2,1)S(1)}, u32[]{:S(2)}) copy-start(bf16[8,640,256]{2,1,0:T(8,128)(2,1)S(1)} %slice.95) | copy-start | bytes 7864324
  621.9 13.3 %copy-start.27 = (f32[10]{0:T(128)S(1)}, f32[10]{0:T(128)}, u32[]{:S(2)}) copy-start(f32[10]{0:T(128)} %copy-done.26) | copy-start | bytes 124
  720.5 236.0 %all-gather.6.cloned.1.call-start = ((), (), s32[]{:S(2)}) async-start(), calls=%async_computation.6 | async-start | bytes 23789568 | tf_op jit(solution)/shard_map/all_gather | solution.py:153
  966.6 20.6 %slice-start = ((s8[16777216]{0:T(1024)(128)(4,1)}), s8[4194304]{0:T(1024)(128)(4,1)S(1)}, s32[]{:S(2)}) async-start(s8[16777216]{0:T(1024)(128)(4,1)} %bitcast.65), calls=%async_computation.9 | async-start | bytes 8388608
  969.8 17.4 %slice-start.1 = ((s8[16777216]{0:T(1024)(128)(4,1)}), s8[4194304]{0:T(1024)(128)(4,1)S(1)}, s32[]{:S(2)}) async-start(s8[16777216]{0:T(1024)(128)(4,1)} %bitcast.65), calls=%async_computation.10 | async-start | bytes 8388608
  969.8 17.4 %slice-start.2 = ((s8[16777216]{0:T(1024)(128)(4,1)}), s8[4194304]{0:T(1024)(128)(4,1)S(1)}, s32[]{:S(2)}) async-start(s8[16777216]{0:T(1024)(128)(4,1)} %bitcast.65), calls=%async_computation.11 | async-start | bytes 8388608
  969.8 17.4 %slice-start.3 = ((s8[16777216]{0:T(1024)(128)(4,1)}), s8[4194304]{0:T(1024)(128)(4,1)S(1)}, s32[]{:S(2)}) async-start(s8[16777216]{0:T(1024)(128)(4,1)} %bitcast.65), calls=%async_computation.12 | async-start | bytes 8388608
  (15 other events, 80.3 us)
Sparse Core Ops, SparseCore 0:
  33.9 55.7 all-reduce.9
  166.7 51.2 all-reduce.11
  239.5 49.6 all-reduce.13
  447.9 38.8 all-reduce.15
  489.0 44.6 all-gather.9
  537.0 58.4 reduce-scatter.1
  720.6 89.6 all-gather.7
  813.1 143.3 all-gather.5

commit v2 on v1

v2 whole, which is shorter than its diff:
```python
import functools

import jax
import jax.numpy as jnp
from jax import lax
from jax.experimental import pallas as pl
from jax.experimental.pallas import tpu as pltpu
from jax.sharding import PartitionSpec as P

ALL_CROPS = 10
GLOBAL_CROPS = 2
SINK_ITERS = 3
TEMP_STUDENT = 0.1
TEMP_TEACHER = 0.04
F32 = jnp.float32
BF16 = jnp.bfloat16
MESH = pl.DeviceIdType.MESH
LOG2E = 1.4426950408889634
CHUNK = 1024
OWN_CHUNK = 512


def gelu_slope(pre):
    cdf = 0.5 * (1.0 + lax.erf(pre * 0.7071067811865476))
    return cdf + pre * jnp.exp(-0.5 * pre * pre) * 0.3989422804014327


def mlp_forward(feats, w_in, b_in, w_mid, b_mid, w_out, b_out):
    pre_one = jnp.dot(feats, w_in, preferred_element_type=F32) + b_in.astype(F32)
    hid_one = jax.nn.gelu(pre_one, approximate=False).astype(BF16)
    pre_two = jnp.dot(hid_one, w_mid, preferred_element_type=F32) + b_mid.astype(F32)
    hid_two = jax.nn.gelu(pre_two, approximate=False).astype(BF16)
    proj = jnp.dot(hid_two, w_out, preferred_element_type=F32) + b_out.astype(F32)
    inv_norm = lax.rsqrt(jnp.sum(proj * proj, axis=-1, keepdims=True))
    unit = proj * inv_norm
    return unit.astype(BF16), proj, (pre_one, hid_one, pre_two, hid_two, unit, inv_norm)


def dot32(a, b):
    return jnp.dot(a, b, preferred_element_type=F32)


def main_kernel(cfg, t_ref, s_ref, pr_hbm, em_hbm, gemb_ref, stats_ref, bown_ref, loss_ref,
                em_v, us_v, e_v, lg_v, gl_v, col_s, col_r, col_a, b_v, srow_v, a_v, f_v, rowm_s, rowm_r, st_s, st_r,
                ld_sem, cs_sem, cr_sem, as_sem, ar_sem, rs_sem, rr_sem, ss_sem, sr_sem):
    n_dp, n_vp, n_proto, n_rows, scale = cfg
    me = lax.axis_index('dp')
    mv = lax.axis_index('vp')
    cb = CHUNK
    local = e_v.shape[1]
    own = local // n_dp
    n_chunk = local // cb
    ns = s_ref.shape[0]
    half = ns // ALL_CROPS
    c_exp = 10.0 * LOG2E
    lanes = cb // 128

    loads = []
    for c in range(n_chunk):
        loads.append((pltpu.make_async_copy(em_hbm.at[:, c * cb:(c + 1) * cb], em_v.at[:, c * cb:(c + 1) * cb], ld_sem.at[0, c]),
                      pltpu.make_async_copy(pr_hbm.at[:, c * cb:(c + 1) * cb], us_v.at[:, c * cb:(c + 1) * cb], ld_sem.at[1, c])))
    for c in range(n_chunk):
        loads[c][0].start()
    for c in range(n_chunk):
        loads[c][1].start()

    barrier = pltpu.get_barrier_semaphore()
    for j in range(1, n_dp):
        pl.semaphore_signal(barrier, inc=1, device_id={'dp': lax.rem(me + j, n_dp)}, device_id_type=MESH)
    for j in range(1, n_vp):
        pl.semaphore_signal(barrier, inc=1, device_id={'vp': lax.rem(mv + j, n_vp)}, device_id_type=MESH)
    pl.semaphore_wait(barrier, n_dp + n_vp - 2)

    def unit_block(ref, off):
        raw = ref[:, pl.ds(off, 128)].astype(F32)
        inv = lax.rsqrt(jnp.sum(raw * raw, axis=0, keepdims=True))
        return (raw * inv).astype(BF16)

    def wait_load(hbm, buf, which, c):
        pltpu.make_async_copy(hbm.at[:, pl.ds(c * cb, cb)], buf.at[:, pl.ds(c * cb, cb)], ld_sem.at[which, c]).wait()

    def teacher_body(c, carry):
        base = pl.multiple_of(c * cb, cb)
        wait_load(em_hbm, em_v, 0, c)
        for l in range(lanes):
            off = pl.multiple_of(base + l * 128, 128)
            em_v[:, pl.ds(off, 128)] = unit_block(em_v, off)
        e = jnp.exp(dot32(t_ref[...], em_v[:, pl.ds(base, cb)]) * (1.0 / TEMP_TEACHER))
        e_v[:, pl.ds(base, cb)] = e
        per = own // cb
        col_s[0, lax.div(c, per), :, pl.ds(pl.multiple_of(lax.rem(c, per) * cb, cb), cb)] = jnp.sum(e, axis=0, keepdims=True)
        return carry

    lax.fori_loop(0, n_chunk, teacher_body, 0)

    def start_cols(it):
        out = []
        for j in range(1, n_dp):
            peer = lax.rem(me + j, n_dp)
            cp = pltpu.make_async_remote_copy(
                src_ref=col_s.at[it, peer], dst_ref=col_r.at[it, me], send_sem=cs_sem.at[it, j], recv_sem=cr_sem.at[it, j],
                device_id={'dp': peer}, device_id_type=MESH)
            cp.start()
            out.append(cp)
        return out

    def finish_cols(it, copies):
        for cp in copies:
            cp.wait()
        tot = col_s[it, me]
        for j in range(1, n_dp):
            tot = tot + col_r[it, lax.rem(me + j, n_dp)]
        col_a[it, me] = tot
        out = []
        for j in range(1, n_dp):
            peer = lax.rem(me + j, n_dp)
            cp = pltpu.make_async_remote_copy(
                src_ref=col_a.at[it, me], dst_ref=col_a.at[it, me], send_sem=as_sem.at[it, j], recv_sem=ar_sem.at[it, j],
                device_id={'dp': peer}, device_id_type=MESH)
            cp.start()
            out.append(cp)
        for cp in out:
            cp.wait()

    def row_partial(it):
        per = own // cb
        for j in range(n_dp):
            inv = 1.0 / (col_a[it, j] * n_proto)
            for h in range(per):
                b_v[j * per + h] = inv[:, h * cb:(h + 1) * cb]

        def body(c, acc):
            for l in range(lanes):
                acc = acc + e_v[:, pl.ds(pl.multiple_of(c * cb + l * 128, 128), 128)] * b_v[c, :, l * 128:(l + 1) * 128]
            return acc
        acc = lax.fori_loop(0, n_chunk, body, jnp.zeros((e_v.shape[0], 128), F32))
        return jnp.sum(acc.T, axis=0, keepdims=True)

    def exchange_rows(it):
        out = []
        for j in range(1, n_vp):
            cp = pltpu.make_async_remote_copy(
                src_ref=rowm_s.at[it], dst_ref=rowm_r.at[it, mv], send_sem=rs_sem.at[it, j], recv_sem=rr_sem.at[it, j],
                device_id={'vp': lax.rem(mv + j, n_vp)}, device_id_type=MESH)
            cp.start()
            out.append(cp)
        for cp in out:
            cp.wait()
        rowm_r[it, mv] = rowm_s[it]
        tot = rowm_r[it, 0]
        for j in range(1, n_vp):
            tot = tot + rowm_r[it, j]
        return tot

    def col_partial(it):
        def body(c, carry):
            per = own // cb
            parts = []
            for l in range(lanes):
                x = e_v[:, pl.ds(pl.multiple_of(c * cb + l * 128, 128), 128)] * a_v[...]
                parts.append(jnp.sum(x, axis=0, keepdims=True))
            col_s[it, lax.div(c, per), :, pl.ds(pl.multiple_of(lax.rem(c, per) * cb, cb), cb)] = jnp.concatenate(parts, axis=1)
            return carry
        lax.fori_loop(0, n_chunk, body, 0)

    def to_column(row):
        return jnp.broadcast_to(row, (128, 128)).T

    copies = start_cols(0)

    srow_v[...] = jnp.zeros_like(srow_v)

    def student_body(c, carry):
        base = pl.multiple_of(c * cb, cb)
        wait_load(pr_hbm, us_v, 1, c)
        for l in range(lanes):
            off = pl.multiple_of(base + l * 128, 128)
            us_v[:, pl.ds(off, 128)] = unit_block(us_v, off)
        lg_v[...] = dot32(s_ref[...], us_v[:, pl.ds(base, cb)])
        for v in range(ALL_CROPS):
            rows = slice(v * half, (v + 1) * half)
            acc = srow_v[rows, :]
            for l in range(lanes):
                acc = acc + jnp.exp2(lg_v[rows, l * 128:(l + 1) * 128] * c_exp)
            srow_v[rows, :] = acc
        return carry

    lax.fori_loop(0, n_chunk, student_body, 0)

    finish_cols(0, copies)
    rowm_s[0, 0:1, :] = row_partial(0)
    n_sg = ns // 128
    for m in range(n_sg):
        rowm_s[0, m + 1:m + 2, :] = jnp.sum(srow_v[m * 128:(m + 1) * 128, :].T, axis=0, keepdims=True)
    tot = jnp.zeros((1, 128), F32)
    for j in range(n_dp):
        for l in range(own // 128):
            tot = tot + col_a[0, j, :, l * 128:(l + 1) * 128]
    rowm_s[0, n_sg + 1:n_sg + 2, :] = tot
    rowm_s[0, n_sg + 2:8, :] = jnp.zeros((8 - n_sg - 2, 128), F32)
    msg = exchange_rows(0)
    total = jnp.sum(msg[n_sg + 1:n_sg + 2, :], axis=1, keepdims=True)
    inv_total = 1.0 / total
    a_row = inv_total / ((msg[0:1, :] * (inv_total * total)) * n_rows)
    row_sum = msg[1:n_sg + 1, :]
    st_s[1:n_sg + 1, :] = row_sum
    st_s[n_sg + 1:8, :] = jnp.zeros((8 - n_sg - 1, 128), F32)
    for it in range(1, SINK_ITERS):
        a_v[...] = to_column(a_row)
        col_partial(it)
        finish_cols(it, start_cols(it))
        rowm_s[it, 0:1, :] = row_partial(it)
        rowm_s[it, 1:8, :] = jnp.zeros((7, 128), F32)
        msg = exchange_rows(it)
        a_row = 1.0 / (msg[0:1, :] * n_rows)
    a_fin = a_row * n_rows
    st_s[0:1, :] = a_fin
    st_copies = []
    for j in range(1, n_dp):
        cp = pltpu.make_async_remote_copy(
            src_ref=st_s, dst_ref=st_r.at[me], send_sem=ss_sem.at[j], recv_sem=sr_sem.at[j],
            device_id={'dp': lax.rem(me + j, n_dp)}, device_id_type=MESH)
        cp.start()
        st_copies.append(cp)
    k_g = scale / TEMP_STUDENT
    a_v[...] = to_column(a_fin * k_g)
    for m in range(n_sg):
        inv_rs = to_column(k_g / st_s[m + 1:m + 2, :])
        cnt0 = GLOBAL_CROPS - 1.0 if 2 * m < GLOBAL_CROPS else GLOBAL_CROPS * 1.0
        f_v[m * 128:(m + 1) * 128, :] = inv_rs * cnt0
    gemb_ref[...] = jnp.zeros_like(gemb_ref)

    def grad_body(c, carry):
        lx, ls0, ls1 = carry
        base = pl.multiple_of(c * cb, cb)
        u = us_v[:, pl.ds(base, cb)]
        lg_v[...] = dot32(s_ref[...], u)
        for l in range(lanes):
            cols = slice(l * 128, (l + 1) * 128)
            off = pl.multiple_of(base + l * 128, 128)
            b = b_v[c, :, cols]
            q0 = e_v[0:half, pl.ds(off, 128)] * a_v[0:half, :] * b
            q1 = e_v[half:2 * half, pl.ds(off, 128)] * a_v[half:2 * half, :] * b
            qs = q0 + q1
            ls0 = ls0 + q0
            ls1 = ls1 + q1
            for v in range(ALL_CROPS):
                rows = slice(v * half, (v + 1) * half)
                t = q1 if v == 0 else (q0 if v == 1 else qs)
                x = lg_v[rows, cols]
                gl_v[rows, cols] = (jnp.exp2(x * c_exp) * f_v[rows, :] - t).astype(BF16)
                lx = lx + t * x
        gemb_ref[...] += lax.dot_general(gl_v[...], u, (((1,), (1,)), ((), ())), preferred_element_type=F32)
        return lx, ls0, ls1

    z = jnp.zeros((half, 128), F32)
    lx, ls0, ls1 = lax.fori_loop(0, n_chunk, grad_body, (z, z, z))
    lpart = lx * (-1.0 / TEMP_STUDENT)
    for m in range(n_sg):
        lrs = to_column(jnp.log(st_s[m + 1:m + 2, :]))
        for h in range(2):
            v = 2 * m + h
            t = ls1 if v == 0 else (ls0 if v == 1 else ls0 + ls1)
            lpart = lpart + t * lrs[h * half:(h + 1) * half, :]
    loss_ref[...] = lpart * (1.0 / k_g * scale)
    bown_ref[...] = 1.0 / (col_a[SINK_ITERS - 1, me] * n_proto)
    for cp in st_copies:
        cp.wait()
    st_r[me] = st_s[...]
    stats_ref[...] = st_r[...]


def own_kernel(cfg, s_ref, st_ref, t_ref, stats_ref, b_ref, pr_ref, em_ref, out_ref, us_v, ut_v, lg_v, gl_v, a_v, f_v, gu_v):
    n_dp, scale = cfg
    own = out_ref.shape[1]
    cb = OWN_CHUNK
    ns = s_ref.shape[1]
    half = ns // ALL_CROPS
    n_sg = ns // 128
    k_g = scale / TEMP_STUDENT
    c_exp = 10.0 * LOG2E

    def unit_body(l, carry):
        off = pl.multiple_of(l * 128, 128)
        for src, dst in ((pr_ref, us_v), (em_ref, ut_v)):
            raw = src[:, pl.ds(off, 128)].astype(F32)
            inv = lax.rsqrt(jnp.sum(raw * raw, axis=0, keepdims=True))
            dst[:, pl.ds(off, 128)] = (raw * inv).astype(BF16)
        gu_v[:, pl.ds(off, 128)] = jnp.zeros((gu_v.shape[0], 128), F32)
        return carry

    lax.fori_loop(0, own // 128, unit_body, 0)

    def group_body(g, carry):
        stats = stats_ref[g]
        a_v[...] = jnp.broadcast_to(stats[0:1, :] * k_g, (128, 128)).T
        for m in range(n_sg):
            cnt0 = GLOBAL_CROPS - 1.0 if 2 * m < GLOBAL_CROPS else GLOBAL_CROPS * 1.0
            f_v[m * 128:(m + 1) * 128, :] = jnp.broadcast_to((k_g * cnt0) / stats[m + 1:m + 2, :], (128, 128)).T

        def chunk_body(c, carry2):
            base = pl.multiple_of(c * cb, cb)
            lg_v[...] = dot32(s_ref[g], us_v[:, pl.ds(base, cb)])
            e = jnp.exp(dot32(t_ref[g], ut_v[:, pl.ds(base, cb)]) * (1.0 / TEMP_TEACHER))
            b_all = b_ref[:, pl.ds(base, cb)]
            for l in range(cb // 128):
                cols = slice(l * 128, (l + 1) * 128)
                b = b_all[:, cols]
                q0 = e[0:half, cols] * a_v[0:half, :] * b
                q1 = e[half:2 * half, cols] * a_v[half:2 * half, :] * b
                qs = q0 + q1
                for v in range(ALL_CROPS):
                    rows = slice(v * half, (v + 1) * half)
                    t = q1 if v == 0 else (q0 if v == 1 else qs)
                    gl_v[rows, cols] = (jnp.exp2(lg_v[rows, cols] * c_exp) * f_v[rows, :] - t).astype(BF16)
            gu_v[:, pl.ds(base, cb)] += dot32(st_ref[g], gl_v[...])
            return carry2

        return lax.fori_loop(0, own // cb, chunk_body, carry)

    lax.fori_loop(0, n_dp, group_body, 0)

    def back_body(l, carry):
        off = pl.multiple_of(l * 128, 128)
        raw = pr_ref[:, pl.ds(off, 128)].astype(F32)
        inv = lax.rsqrt(jnp.sum(raw * raw, axis=0, keepdims=True))
        unit = raw * inv
        gu = gu_v[:, pl.ds(off, 128)]
        out_ref[:, pl.ds(off, 128)] = (gu - unit * jnp.sum(unit * gu, axis=0, keepdims=True)) * inv
        return carry

    lax.fori_loop(0, own // 128, back_body, 0)


def solution(mesh):
    vp_size = mesh.shape['vp']
    dp_size = mesh.shape['dp']

    def local_step(student_x, teacher_x, w_in, b_in, w_mid, b_mid, w_out, b_out, protos,
                   ema_w_in, ema_b_in, ema_w_mid, ema_b_mid, ema_w_out, ema_b_out, ema_protos):
        n_img = student_x.shape[0] // ALL_CROPS
        local_proto = protos.shape[1]
        n_proto = local_proto * vp_size
        n_rows = GLOBAL_CROPS * n_img * dp_size
        hidden = w_mid.shape[0]
        bott = w_out.shape[1]
        in_dim = w_in.shape[0]
        i_dp = lax.axis_index('dp')
        i_vp = lax.axis_index('vp')
        scale = 1.0 / (n_img * dp_size * GLOBAL_CROPS * (ALL_CROPS - 1))

        n_s = student_x.shape[0]
        n_t = teacher_x.shape[0]
        own = local_proto // dp_size
        student_x = student_x.reshape(n_img, ALL_CROPS, in_dim).swapaxes(0, 1).reshape(n_s, in_dim)
        teacher_x = teacher_x.reshape(n_img, GLOBAL_CROPS, in_dim).swapaxes(0, 1).reshape(n_t, in_dim)
        t_emb, t_proj, _ = mlp_forward(teacher_x, ema_w_in, ema_b_in, ema_w_mid, ema_b_mid, ema_w_out, ema_b_out)
        s_emb, s_proj, saved = mlp_forward(student_x, w_in, b_in, w_mid, b_mid, w_out, b_out)
        emb_all = lax.all_gather(jnp.concatenate([s_proj, t_proj], axis=0), 'dp', axis=0)
        emb_all = (emb_all * lax.rsqrt(jnp.sum(emb_all * emb_all, axis=-1, keepdims=True))).astype(BF16)

        sem = pltpu.SemaphoreType.DMA
        it = SINK_ITERS
        n_chunk = local_proto // CHUNK
        vm = pl.BlockSpec(memory_space=pltpu.VMEM)
        g_emb_part, stats, b_own, loss_part = pl.pallas_call(
            functools.partial(main_kernel, (dp_size, vp_size, float(n_proto), float(n_rows), scale)),
            out_shape=(jax.ShapeDtypeStruct((n_s, bott), F32), jax.ShapeDtypeStruct((dp_size, 8, 128), F32),
                       jax.ShapeDtypeStruct((1, own), F32), jax.ShapeDtypeStruct((n_img, 128), F32)),
            in_specs=[vm, vm, pl.BlockSpec(memory_space=pltpu.HBM), pl.BlockSpec(memory_space=pltpu.HBM)],
            out_specs=(vm, vm, vm, vm),
            scratch_shapes=[
                pltpu.VMEM((bott, local_proto), BF16), pltpu.VMEM((bott, local_proto), BF16),
                pltpu.VMEM((n_t, local_proto), F32), pltpu.VMEM((n_s, CHUNK), F32), pltpu.VMEM((n_s, CHUNK), BF16),
                pltpu.VMEM((it, dp_size, 1, own), F32), pltpu.VMEM((it, dp_size, 1, own), F32),
                pltpu.VMEM((it, dp_size, 1, own), F32), pltpu.VMEM((n_chunk, 1, CHUNK), F32),
                pltpu.VMEM((n_s, 128), F32), pltpu.VMEM((n_t, 128), F32), pltpu.VMEM((n_s, 128), F32),
                pltpu.VMEM((it, 8, 128), F32), pltpu.VMEM((it, vp_size, 8, 128), F32),
                pltpu.VMEM((8, 128), F32), pltpu.VMEM((dp_size, 8, 128), F32),
                sem((2, n_chunk)), sem((it, dp_size)), sem((it, dp_size)), sem((it, dp_size)), sem((it, dp_size)),
                sem((it, vp_size)), sem((it, vp_size)), sem((dp_size,)), sem((dp_size,))],
            compiler_params=pltpu.CompilerParams(collective_id=0, has_side_effects=True, vmem_limit_bytes=60 * 1024 * 1024),
            cost_estimate=pl.CostEstimate(flops=18 * 10 ** 9, bytes_accessed=20 * 10 ** 6, transcendentals=25 * 10 ** 6),
            name='sinkhorn_student',
        )(t_emb, s_emb, protos, ema_protos)
        g_emb = lax.psum(g_emb_part, 'vp')
        loss_part = jnp.sum(loss_part)

        c0 = i_dp * own
        s_all = emb_all[:, :n_s]
        gp_own = pl.pallas_call(
            functools.partial(own_kernel, (dp_size, scale)),
            out_shape=jax.ShapeDtypeStruct((bott, own), F32),
            in_specs=[vm] * 7, out_specs=vm,
            scratch_shapes=[pltpu.VMEM((bott, own), BF16), pltpu.VMEM((bott, own), BF16), pltpu.VMEM((n_s, OWN_CHUNK), F32),
                            pltpu.VMEM((n_s, OWN_CHUNK), BF16), pltpu.VMEM((n_t, 128), F32), pltpu.VMEM((n_s, 128), F32),
                            pltpu.VMEM((bott, own), F32)],
            compiler_params=pltpu.CompilerParams(vmem_limit_bytes=48 * 1024 * 1024),
            cost_estimate=pl.CostEstimate(flops=12 * 10 ** 9, bytes_accessed=12 * 10 ** 6, transcendentals=12 * 10 ** 6),
            name='own_columns',
        )(s_all, s_all.swapaxes(1, 2), emb_all[:, n_s:], stats, b_own,
          lax.dynamic_slice_in_dim(protos, c0, own, axis=1), lax.dynamic_slice_in_dim(ema_protos, c0, own, axis=1))
        g_protos = lax.all_gather(gp_own, 'dp', axis=1, tiled=True)

        pre_one, hid_one, pre_two, hid_two, unit, inv_norm = saved
        qh = hidden // vp_size
        h0 = i_vp * qh
        g_proj = (g_emb - unit * jnp.sum(unit * g_emb, axis=-1, keepdims=True)) * inv_norm
        g_proj_lo = g_proj.astype(BF16)
        g_hid_two = jnp.einsum('nb,hb->nh', g_proj_lo, w_out, preferred_element_type=F32)
        g_pre_two = g_hid_two * gelu_slope(pre_two)
        g_pre_two_lo = g_pre_two.astype(BF16)
        hid_two_q = lax.dynamic_slice_in_dim(hid_two, h0, qh, axis=1)
        hid_one_q = lax.dynamic_slice_in_dim(hid_one, h0, qh, axis=1)
        pre_one_q = lax.dynamic_slice_in_dim(pre_one, h0, qh, axis=1)
        w_mid_q = lax.dynamic_slice_in_dim(w_mid, h0, qh, axis=0)
        g_w_out_q = jnp.einsum('nh,nb->hb', hid_two_q, g_proj_lo, preferred_element_type=F32)
        g_w_mid_q = jnp.einsum('ng,nh->gh', hid_one_q, g_pre_two_lo, preferred_element_type=F32)
        g_hid_one_q = jnp.einsum('nh,gh->ng', g_pre_two_lo, w_mid_q, preferred_element_type=F32)
        g_pre_one_q = g_hid_one_q * gelu_slope(pre_one_q)
        g_w_in_q = jnp.einsum('nh,nf->hf', g_pre_one_q.astype(BF16), student_x, preferred_element_type=F32)
        bq = bott // vp_size
        gb_in = jnp.sum(g_pre_one_q, axis=0)
        gb_mid = lax.dynamic_slice_in_dim(jnp.sum(g_pre_two, axis=0), h0, qh, axis=0)
        gb_out = lax.dynamic_slice_in_dim(jnp.sum(g_proj, axis=0), i_vp * bq, bq, axis=0)
        tail = jnp.stack([gb_in, gb_mid, jnp.pad(gb_out, (0, qh - bq)),
                          jnp.pad(loss_part.reshape(1), (0, qh - 1))], axis=1)
        stack = jnp.concatenate([g_w_mid_q, g_w_in_q, g_w_out_q, jnp.pad(tail, ((0, 0), (0, 124)))], axis=1)
        part = lax.psum_scatter(stack, 'dp', scatter_dimension=0, tiled=True)
        full = lax.all_gather(part, ('vp', 'dp'), axis=0, tiled=True)
        e1 = hidden
        e2 = e1 + in_dim
        e3 = e2 + bott
        tails = full[:, e3:]
        loss = jnp.sum(tails.reshape(vp_size, qh, 128)[:, 0, 3])
        o_b_out = tails.reshape(vp_size, qh, 128)[:, :bq, 2].reshape(bott)
        return (loss, full[:, e1:e2].T, tails[:, 0], full[:, :e1], tails[:, 1], full[:, e2:e3], o_b_out, g_protos)

    by_rows = P('dp', None)
    by_cols = P(None, 'vp')
    replicated = P()
    head_specs = (replicated,) * 6
    in_specs = (by_rows, by_rows) + head_specs + (by_cols,) + head_specs + (by_cols,)
    out_specs = (replicated,) * 7 + (by_cols,)
    return jax.shard_map(local_step, mesh=mesh, in_specs=in_specs, out_specs=out_specs, check_vma=False)
```

time: 1010 us -> 559 us (0.55)
  other arithmetic: 212 us -> 17 us
  local copies, waits for them, and re-layouts: 244 us -> 51 us
  Pallas kernels: 0 us -> 130 us
  matrix products: 137 us -> 60.8 us
  waiting for transfers between devices: 339 us -> 283 us
  blocking collectives: 51.5 us -> 0 us
    reshape x5 -> x2, local copies, waits for them, and re-layouts: 144 us -> 2.34 us  [the longest x1 1.41 us: local_step(): student_x.reshape(n_img, ALL_CROPS, in_dim).swapaxes(0, 1)]
    pallas_call x0 -> x2, Pallas kernels: none -> 130 us  [the longest x1 95.1 us: local_step(): pl.pallas_call(functools.partial(main_kernel, (dp_size, vp_size, float(n_...]
    convert_element_type x3, other arithmetic: 94.6 us -> 2.58 us  [the longest x2 1.6 us: mlp_forward(): unit.astype(BF16)]
    dot_general x6 -> x0, matrix products: 78.8 us -> none  [the longest x1 19.9 us: local_step(): logits = jnp.dot(s_emb, s_unit, preferred_element_type=F32) / TEMP_STUDENT]
    convert_element_type x2 -> x0, local copies, waits for them, and re-layouts: 60.2 us -> none  [grad_logits(): return (g.reshape(nr, kk).astype(BF16), targets)]
    reduce_sum x11 -> x1, other arithmetic: 61.6 us -> 1.37 us  [local_step(): loss_part = jnp.sum(loss_part)]
    psum x3 -> x0, blocking collectives: 42.9 us -> none  [the longest x1 22.9 us: local_step(): packed = lax.psum(jnp.concatenate([rows, srow, tot], axis=0), 'vp')]
    psum x4 -> x1, waiting for transfers between devices: 76.5 us -> 36.8 us  [local_step(): g_emb = lax.psum(g_emb_part, 'vp')]
  transfers between devices with their start and end apart: 8 -> 5, of which waited for: 5 -> 4; matrix products, arithmetic and copies ran while one was open for 37% -> 7% of each run, Pallas kernels for 0% -> 6%
where the time goes in v2:
time: 559 us
  waiting for transfers between devices  283 us (51%)
  Pallas kernels  130 us (23%)
  matrix products  60.8 us (11%)
  local copies, waits for them, and re-layouts  51 us (9%)
  other arithmetic  17 us (3%)
  between operations  16 us (3%)
    all_gather x1, waiting for transfers between devices, local_step(): full = lax.all_gather(part, ('vp', 'dp'), axis=0, tiled=True)  146 us
    pallas_call x1, Pallas kernels, local_step(): pl.pallas_call(functools.partial(main_kernel, (dp_size, vp_size, float(n_...  95.1 us
    all_gather x1, waiting for transfers between devices, local_step(): g_protos = lax.all_gather(gp_own, 'dp', axis=1, tiled=True)  91.9 us
    psum x1, waiting for transfers between devices, local_step(): g_emb = lax.psum(g_emb_part, 'vp')  36.8 us
    pallas_call x1, Pallas kernels, local_step(): pl.pallas_call(functools.partial(own_kernel, (dp_size, scale)), out_shape...  35 us
    dot_general x2, matrix products, mlp_forward(): jnp.dot(hid_one, w_mid, preferred_element_type=F32) + b_mid.astype(F32)  30.3 us
    dot_general x1, matrix products, mlp_forward(): jnp.dot(feats, w_in, preferred_element_type=F32) + b_in.astype(F32)  13.7 us
    slice x1, local copies, waits for them, and re-layouts, local_step(): full[:, :e1]  13.6 us
  transfers between devices with their start and end apart: 5, of which 4 were waited for; matrix products, arithmetic and copies ran while one was open for 7% of the time, Pallas kernels for 6%

profile of v2, /device:TPU:0, one launch (start us, length us, event | category | flops | bytes accessed | tf_op | source)
XLA Modules:
  0.0 558.6 jit_solution(15855332937469127950)
XLA Ops:
  11.2 10.1 %fusion.42 = bf16[128,2048]{1,0:T(8,128)(2,1)S(1)} fusion(bf16[2048,2048]{1,0:T(8,128)(2,1)} %param.27, bf16[128,384]{1,0:T(8,128)(2,1)S(1)} %bitcast.43, bf16[384,2048]{1,0:T(8,128)(2,1)} %param.25, f32[2048]{0:T(1024)S(1)} %convert_element_type.58, f32[2048]{0:T(1024)S(1)} %convert_element_type.56), kind=kOutput, calls=%fused_computation.72 | convolution fusion | flops 1309671424 | bytes 10600448 | tf_op jit(solution)/shard_map/dot_general | solution.py:31
  21.7 1.4 reshape.54
  23.3 13.7 %fusion.2 = (bf16[640,2048]{1,0:T(8,128)(2,1)S(1)}, f32[640,2048]{1,0:T(8,128)}) fusion(f32[2048]{0:T(1024)S(1)} %convert_element_type.54, bf16[640,384]{1,0:T(8,128)(2,1)S(1)} %bitcast.38, bf16[384,2048]{1,0:T(8,128)(2,1)S(1)} %copy-done), kind=kOutput, calls=%fused_computation.9 | convolution fusion | flops 1093140480 | bytes 9936896 | tf_op jit(solution)/shard_map/dot_general | solution.py:29
  37.0 20.2 %fusion.5 = (bf16[640,2048]{1,0:T(8,128)(2,1)S(1)}, f32[640,2048]{1,0:T(8,128)}) fusion(f32[2048]{0:T(1024)S(1)} %convert_element_type.62, bf16[640,2048]{1,0:T(8,128)(2,1)S(1)} %get-tuple-element.56, bf16[2048,2048]{1,0:T(8,128)(2,1)} %param.20), kind=kOutput, calls=%fused_computation.12 | convolution fusion | flops 5455216640 | bytes 18882560 | tf_op jit(solution)/shard_map/dot_general | solution.py:31
  57.2 1.5 copy-done.8
  61.3 95.1 %sinkhorn_student.1 = (f32[640,256]{1,0:T(8,128)}, f32[8,8,128]{2,1,0:T(8,128)}, f32[1,2048]{1,0:T(1,128)}, f32[64,128]{1,0:T(8,128)}) custom-call(bf16[128,256]{1,0:T(8,128)(2,1)} %multiply_convert_fusion.2.t_ref, bf16[640,256]{1,0:T(8,128)(2,1)} %multiply_convert_fusion.1.s_ref, bf16[256,16384]{1,0:T(8,128)(2,1)} %pr_hbm.1, bf16[256,16384]{1,0:T(8,128)(2,1)} %em_hbm.1), custom_call_target="tpu_custom_call" | custom-call | flops 17999998976 | bytes 20000000 | tf_op jit(solution)/shard_map/sinkhorn_student/pallas_call | solution.py:366
  156.4 0.9 pad_maximum_fusion
  157.5 1.4 reduce_sum.87
  159.5 36.8 %all-reduce.5.cloned.1.call-done = f32[640,256]{1,0:T(8,128)} async-done(((f32[640,256]{1,0:T(8,128)}), f32[640,256]{1,0:T(8,128)}) %all-reduce.5.cloned.1.call-update) | async-done | bytes 655376 | tf_op jit(solution)/shard_map/psum | solution.py:386
  196.3 1.4 multiply_reduce_fusion.1
  197.7 1.3 fusion.128
  199.1 5.5 fusion.129
  204.7 4.7 fusion.130
  209.6 1.7 fusion.57
  211.9 2.9 fusion.35
  214.8 2.8 select_maximum_fusion
  217.7 1.7 constant_dynamic-slice_fusion
  219.5 3.8 multiply_reduce_fusion
  224.1 1.0 multiply_convert_fusion
  225.1 2.9 slice_bitcast_fusion.1
  228.0 4.4 copy.55.st_ref
  232.4 35.0 %own_columns.1 = f32[256,2048]{1,0:T(8,128)} custom-call(bf16[8,640,256]{2,1,0:T(8,128)(2,1)} %get-tuple-element.53.s_ref, bf16[8,256,640]{2,1,0:T(8,128)(2,1)} %copy.55.st_ref, bf16[8,128,256]{2,1,0:T(8,128)(2,1)S(1)} %slice.51.t_ref, f32[8,8,128]{2,1,0:T(8,128)S(1)} %copy-done.2, f32[1,2048]{1,0:T(1,128)S(1)} %copy-done.3, ...), custom_call_target="tpu_custom_call" | custom-call | flops 12000000000 | bytes 12000000 | tf_op jit(solution)/shard_map/own_columns/pallas_call | solution.py:391
  267.5 8.3 %reduce-scatter.2.cloned.1.call-done = f32[64,2816]{1,0:T(8,128)} async-done(((f32[512,2816]{1,0:T(8,128)}), f32[64,2816]{1,0:T(8,128)}) %reduce-scatter.2.cloned.1.call-update) | async-done | bytes 720912 | tf_op jit(solution)/shard_map/reduce_scatter | solution.py:429
  275.8 91.9 %all-gather.7.cloned.1.call-done = f32[256,16384]{1,0:T(8,128)} async-done(((f32[256,2048]{1,0:T(8,128)}), f32[256,16384]{1,0:T(8,128)}) %all-gather.7.cloned.1.call-update) | async-done | bytes 16777232 | tf_op jit(solution)/shard_map/all_gather | solution.py:403
  367.8 146.2 %all-gather.5.cloned.1.call-done = f32[2048,2816]{1,0:T(8,128)} async-done(((f32[64,2816]{1,0:T(8,128)}), f32[2048,2816]{1,0:T(8,128)}) %all-gather.5.cloned.1.call-update) | async-done | bytes 23068688 | tf_op jit(solution)/shard_map/all_gather | solution.py:430
  514.0 1.3 slice.42
  516.2 3.8 slice_bitcast_fusion
  520.0 3.5 copy.56
  524.2 3.2 slice_reduce_fusion
  527.4 13.6 %slice.46 = f32[2048,2048]{1,0:T(8,128)} slice(f32[2048,2816]{1,0:T(8,128)} %all-gather.5.cloned.1.call-done), slice={[0:2048], [0:2048]} | slice | bytes 33554432 | tf_op jit(solution)/shard_map/slice | solution.py:437
  541.0 3.8 slice.48
  544.8 6.2 %copy.62 = f32[256,16384]{1,0:T(8,128)} copy(f32[256,16384]{1,0:T(8,128)S(1)} %bitcast.36) | data formatting | bytes 33554432
  (74 shorter events, 10.4 us)
Async XLA Ops:
  8.0 15.3 %copy-start = (bf16[384,2048]{1,0:T(8,128)(2,1)S(1)}, bf16[384,2048]{1,0:T(8,128)(2,1)}, u32[]{:S(2)}) copy-start(bf16[384,2048]{1,0:T(8,128)(2,1)} %param.18) | copy-start | bytes 4718596
  8.0 188.3 %all-reduce.5.cloned.1.call-start = ((), (), s32[]{:S(2)}) async-start(), calls=%async_computation.1 | async-start | bytes 1310720 | tf_op jit(solution)/shard_map/psum | solution.py:386
  11.2 10.1 %copy-start.7 = (bf16[2048,256]{1,0:T(8,128)(2,1)S(1)}, bf16[2048,256]{1,0:T(8,128)(2,1)}, u32[]{:S(2)}) copy-start(bf16[2048,256]{1,0:T(8,128)(2,1)} %param.29) | copy-start | bytes 3145732
  11.2 10.5 %copy-start.13 = (bf16[256]{0:T(256)(128)(2,1)S(1)}, bf16[256]{0:T(256)(128)(2,1)}, u32[]{:S(2)}) copy-start(bf16[256]{0:T(256)(128)(2,1)} %param.23) | copy-start | bytes 1540
  11.2 10.5 %copy-start.10 = (bf16[2048]{0:T(1024)(128)(2,1)S(1)}, bf16[2048]{0:T(1024)(128)(2,1)}, u32[]{:S(2)}) copy-start(bf16[2048]{0:T(1024)(128)(2,1)} %param.21) | copy-start | bytes 12292
  11.2 10.5 %copy-start.11 = (bf16[2048]{0:T(1024)(128)(2,1)S(1)}, bf16[2048]{0:T(1024)(128)(2,1)}, u32[]{:S(2)}) copy-start(bf16[2048]{0:T(1024)(128)(2,1)} %param.19) | copy-start | bytes 12292
  37.0 20.2 %copy-start.9 = (bf16[640,2048]{1,0:T(8,128)(2,1)}, bf16[640,2048]{1,0:T(8,128)(2,1)S(1)}, u32[]{:S(2)}) copy-start(bf16[640,2048]{1,0:T(8,128)(2,1)S(1)} %get-tuple-element.56) | copy-start | bytes 7864324
  37.0 21.7 %copy-start.12 = (bf16[2048,256]{1,0:T(8,128)(2,1)S(1)}, bf16[2048,256]{1,0:T(8,128)(2,1)}, u32[]{:S(2)}) copy-start(bf16[2048,256]{1,0:T(8,128)(2,1)} %param.22) | copy-start | bytes 3145732
  57.2 1.5 copy-start.8
  156.4 63.1 %all-gather.9.cloned.1.call-start = ((), (), s32[]{:S(2)}) async-start(), calls=%async_computation.5 | async-start | bytes 7077888 | tf_op jit(solution)/shard_map/all_gather | solution.py:359
  157.4 118.4 %reduce-scatter.2.cloned.1.call-start = ((), (), s32[]{:S(2)}) async-start(), calls=%async_computation.2 | async-start | bytes 6488064 | tf_op jit(solution)/shard_map/reduce_scatter | solution.py:429
  204.6 4.8 copy-start.5
  209.6 2.3 copy-start.6
  217.6 150.2 %all-gather.7.cloned.1.call-start = ((), (), s32[]{:S(2)}) async-start(), calls=%async_computation.4 | async-start | bytes 18874368 | tf_op jit(solution)/shard_map/all_gather | solution.py:403
  219.5 4.6 copy-start.4
  225.1 7.3 %copy-start.2 = (f32[8,8,128]{2,1,0:T(8,128)S(1)}, f32[8,8,128]{2,1,0:T(8,128)}, u32[]{:S(2)}) copy-start(f32[8,8,128]{2,1,0:T(8,128)} %get-tuple-element.14.stats_ref) | copy-start | bytes 98308
  225.1 7.3 %copy-start.3 = (f32[1,2048]{1,0:T(1,128)S(1)}, f32[1,2048]{1,0:T(1,128)}, u32[]{:S(2)}) copy-start(f32[1,2048]{1,0:T(1,128)} %get-tuple-element.15.b_ref) | copy-start | bytes 24580
  267.5 246.5 %all-gather.5.cloned.1.call-start = ((), (), s32[]{:S(2)}) async-start(), calls=%async_computation.3 | async-start | bytes 23789568 | tf_op jit(solution)/shard_map/all_gather | solution.py:430
  524.2 20.6 %slice-start = ((s8[16777216]{0:T(1024)(128)(4,1)}), s8[4194304]{0:T(1024)(128)(4,1)S(1)}, s32[]{:S(2)}) async-start(s8[16777216]{0:T(1024)(128)(4,1)} %bitcast.35), calls=%async_computation.6 | async-start | bytes 8388608
  527.4 17.4 %slice-start.1 = ((s8[16777216]{0:T(1024)(128)(4,1)}), s8[4194304]{0:T(1024)(128)(4,1)S(1)}, s32[]{:S(2)}) async-start(s8[16777216]{0:T(1024)(128)(4,1)} %bitcast.35), calls=%async_computation.7 | async-start | bytes 8388608
  527.4 17.4 %slice-start.2 = ((s8[16777216]{0:T(1024)(128)(4,1)}), s8[4194304]{0:T(1024)(128)(4,1)S(1)}, s32[]{:S(2)}) async-start(s8[16777216]{0:T(1024)(128)(4,1)} %bitcast.35), calls=%async_computation.8 | async-start | bytes 8388608
  527.4 17.4 %slice-start.3 = ((s8[16777216]{0:T(1024)(128)(4,1)}), s8[4194304]{0:T(1024)(128)(4,1)S(1)}, s32[]{:S(2)}) async-start(s8[16777216]{0:T(1024)(128)(4,1)} %bitcast.35), calls=%async_computation.9 | async-start | bytes 8388608
  544.8 6.2 %copy-start.1 = (bf16[384,2048]{1,0:T(8,128)(2,1)S(1)}, bf16[384,2048]{1,0:T(8,128)(2,1)}, u32[]{:S(2)}) copy-start(bf16[384,2048]{1,0:T(8,128)(2,1)} %param.18) | copy-start | bytes 4718596
Sparse Core Ops, SparseCore 0:
  156.5 39.7 all-reduce.4
Sparse Core Ops, SparseCore 1:
  159.3 44.0 all-gather.8
  217.7 58.1 reduce-scatter.1
  278.2 89.6 all-gather.6
  370.7 143.3 all-gather.4
